TPU v7x, 128 devices: a whole 4x4x4 slice. The times are simulated.
128 devices in a mesh: px: 8 (over z_hi, y), py: 16 (over x, z_lo, core).
Axes of the slice: x: 4, y: 4, z: 4 (z_hi: 2, z_lo: 2; z = z_hi * 2 + z_lo), core: 2. Of those that a mesh axis runs over, the one named last changes fastest.
Arguments:
- white_noise: float32 [2, 128, 512, 256], P(None, 'px', 'py'), may hold values from -6 to 6
- spectrum: float32 [128, 512, 256], P('px', 'py'), may hold values from 0.1 to 2, as said below
- group_table: int32 [3, 16], replicated, may hold values from 0 to 15, each once within a row
Outputs:
- modulus: float32 [2, 128, 512, 256], P(None, 'px', 'py')
- level_one: float32 [2, 64, 256, 128], P(None, 'px', 'py')
- level_two: float32 [2, 32, 128, 64], P(None, 'px', 'py')
- level_three: float32 [2, 16, 64, 32], P(None, 'px', 'py')
Inputs may be any that keep to these rules, and one draw needn't show every extreme that they name: spectrum[j, m, k] equals spectrum[(128 - j) % 128, (512 - m) % 512, (256 - k) % 256]. `group_table`: each row is a permutation of 0 to 15.
All inputs are finite; a program needn't handle non-finite values.
Results may differ from a plain program's by a relative error of at most 0.000088.
Values sent between devices are 32-bit elements; how exact they have to be, the bound alone decides.
A program may use at most 192 MiB of HBM per device.

v0:
```python
import math

import jax
import jax.numpy as jnp
from jax import lax
from jax.sharding import Mesh
from jax.sharding import PartitionSpec as P

PX = ("px_0", "px_1")
PY = ("py_0", "py_1", "py_2")
PX_PY = ("px_0", "px_1", "py_0", "py_1", "py_2")


def in_blocks(x, dim, size):
    before, after = (x.shape[:dim], x.shape[dim + 1 :])
    return jnp.moveaxis(x.reshape(*before, size, -1, *after), dim, 0)


def joined_along(blocks, dim):
    shape = list(blocks.shape[1:])
    shape[dim] *= blocks.shape[0]
    return jnp.moveaxis(blocks, 0, dim).reshape(shape)


def moved_by_axis(blocks, axes, order):
    inside = blocks.shape[1:]
    whole = blocks.reshape(*(lax.axis_size(a) for a in axes), *inside)
    for k in order:
        whole = lax.all_to_all(whole, axes[k], k, k, tiled=True)
    return whole.reshape(-1, *inside)


def core_and_chips(x, groups, order, split_dim, concat_dim):
    size = lax.axis_size(groups[0]) * lax.axis_size(groups[1])
    blocks = in_blocks(x, split_dim, size)
    return joined_along(moved_by_axis(blocks, groups, order), concat_dim)


def gather_together(arrays, axis, dims):
    line = jnp.concatenate([a.reshape(-1) for a in arrays])
    lines, at, gathered = (lax.all_gather(line, axis), 0, [])
    for a, dim in zip(arrays, dims):
        blocks = lines[:, at : at + a.size].reshape(-1, *a.shape)
        gathered.append(joined_along(blocks, dim))
        at += a.size
    return tuple(gathered)


def dft_tables(length, direction):
    positions = lax.iota(jnp.int32, length)
    products = positions[:, None] * positions[None, :] % length
    angles = products.astype(jnp.float32) * (2.0 * math.pi / length)
    return (jnp.cos(angles), direction * jnp.sin(angles))


def complex_apply(stacked, table_cos, table_sin, pattern):
    half_count = stacked.shape[0] // 2
    real_part = stacked[:half_count]
    imag_part = stacked[half_count:]
    real_cos = jnp.einsum(pattern, real_part, table_cos, precision=lax.Precision.HIGHEST)
    imag_sin = jnp.einsum(pattern, imag_part, table_sin, precision=lax.Precision.HIGHEST)
    imag_cos = jnp.einsum(pattern, imag_part, table_cos, precision=lax.Precision.HIGHEST)
    real_sin = jnp.einsum(pattern, real_part, table_sin, precision=lax.Precision.HIGHEST)
    return jnp.concatenate([real_cos - imag_sin, imag_cos + real_sin], 0)


def forward(payload, direction, carried_count):
    leading, length_z, cells_x, cells_y = payload.shape
    size_px = lax.axis_size(PX)
    size_py = lax.axis_size(PY)
    length_x = size_px * cells_x
    length_y = size_py * cells_y
    kept = leading - carried_count
    y_cos, y_sin = dft_tables(length_y, direction)
    x_cos, x_sin = dft_tables(length_x, direction)
    devices_all = size_px * size_py
    part_z = length_z // devices_all
    flat = payload.reshape(leading, length_z, cells_x * cells_y)
    received = lax.all_to_all(flat, PX_PY, split_axis=1, concat_axis=2, tiled=True)
    received = received.reshape(leading, part_z, size_px, size_py, cells_x, cells_y)
    along_y = complex_apply(
        received[:kept],
        y_cos.reshape(size_py, cells_y, length_y),
        y_sin.reshape(size_py, cells_y, length_y),
        "lkpqxb,qbm->lkpxm",
    )
    spectral = complex_apply(
        along_y,
        x_cos.reshape(size_px, cells_x, length_x),
        x_sin.reshape(size_px, cells_x, length_x),
        "lkpxm,pxj->lkjm",
    )
    carried = jnp.transpose(received[kept:], (0, 1, 2, 4, 3, 5)).reshape(
        carried_count, part_z, length_x, length_y
    )
    return (spectral, carried)


def backward(spectral, direction):
    leading, part_z, length_x, length_y = spectral.shape
    size_px = lax.axis_size(PX)
    size_py = lax.axis_size(PY)
    cells_x = length_x // size_px
    cells_y = length_y // size_py
    x_cos, x_sin = dft_tables(length_x, direction)
    y_cos, y_sin = dft_tables(length_y, direction)
    devices_all = size_px * size_py
    along_x = complex_apply(
        spectral,
        x_cos.reshape(length_x, size_px, cells_x),
        x_sin.reshape(length_x, size_px, cells_x),
        "lkjm,jpx->lkpxm",
    )
    arranged = complex_apply(
        along_x,
        y_cos.reshape(length_y, size_py, cells_y),
        y_sin.reshape(length_y, size_py, cells_y),
        "lkpxm,mqb->lkpqxb",
    )
    arranged = arranged.reshape(leading, part_z, devices_all * cells_x * cells_y)
    received = core_and_chips(arranged, (("px_0", "px_1", "py_0", "py_1"), "py_2"), (1, 0), 2, 1)
    return received.reshape(leading, devices_all * part_z, cells_x, cells_y)


def coarsen(values):
    members, size_x, size_y, size_z = values.shape
    blocks = values.reshape(members, size_x // 2, 2, size_y // 2, 2, size_z // 2, 2)
    return blocks.mean(axis=(2, 4, 6))


def on_device(white_noise, spectrum, group_table):
    members, cells_x, cells_y, length_z = white_noise.shape
    length_x = cells_x * lax.axis_size(PX)
    length_y = cells_y * lax.axis_size(PY)
    z_cos, z_sin = dft_tables(length_z, -1.0)
    paired = complex_apply(white_noise, z_cos, z_sin, "fxyz,zk->fkxy")
    spectrum_rows = jnp.transpose(spectrum, (2, 0, 1))[None]
    inverse_cos, inverse_sin = dft_tables(length_z, 1.0)
    payload = jnp.concatenate([paired, spectrum_rows], 0)
    spectral, carried = forward(payload, -1.0, 1)
    restored = backward(spectral * carried, 1.0)
    fields = complex_apply(restored, inverse_cos, inverse_sin, "lkxy,kz->lxyz")
    fields = fields * (1.0 / (length_x * length_y * length_z))
    modulus = jnp.exp(0.5 * fields)
    coarse_one = coarsen(modulus)
    coarse_two = coarsen(coarse_one)
    coarse_three = coarsen(coarse_two)
    gathered = gather_together((coarse_one, coarse_two, coarse_three), PY, (2, 2, 2))
    column = lax.axis_index(PY)
    routed = []
    for level_index in range(3):
        width = gathered[level_index].shape[2] // lax.axis_size(PY)
        source_row = group_table[level_index, column]
        routed.append(lax.dynamic_slice_in_dim(gathered[level_index], source_row * width, width, 2))
    return (modulus, routed[0], routed[1], routed[2])


def solution(mesh):
    split = Mesh(mesh.devices.reshape(2, 4, 4, 2, 2), ("px_0", "px_1", "py_0", "py_1", "py_2"))
    placed = (P(None, PX, PY, None), P(PX, PY, None), P())
    return jax.shard_map(
        on_device,
        mesh=split,
        in_specs=placed,
        out_specs=(
            P(None, PX, PY, None),
            P(None, PX, PY, None),
            P(None, PX, PY, None),
            P(None, PX, PY, None),
        ),
        check_vma=False,
    )
```

profile of v0, /device:TPU:1, one launch (start us, length us, event | category | flops | bytes accessed | tf_op | source)
XLA Modules:
  0.0 350.6 jit_solution(2391356412556793110)
XLA Ops:
  7.2 2.7 fusion.41
  9.9 2.7 fusion.37
  17.9 11.5 %all-to-all-start = ((f32[3,256,512]{2,0,1:T(4,128)}), f32[3,256,512]{2,0,1:T(4,128)S(1)}, u32[]{:S(2)}, u32[]{:S(2)}) async-start(f32[3,256,512]{2,0,1:T(4,128)} %copy.71), calls=%async_computation | async-start | bytes 4194304 | tf_op jit(solution)/shard_map/all_to_all | solution.py:79
  29.7 29.4 %all-to-all-done = f32[3,256,512]{2,0,1:T(4,128)S(1)} async-done(((f32[3,256,512]{2,0,1:T(4,128)}), f32[3,256,512]{2,0,1:T(4,128)S(1)}, u32[]{:S(2)}, u32[]{:S(2)}) %all-to-all-start) | async-done | bytes 1572896 | tf_op jit(solution)/shard_map/all_to_all | solution.py:79
  63.8 6.0 %convolution_bitcast_fusion.3 = f32[2,8,16,512]{3,2,1,0:T(8,128)S(1)} fusion(f32[2,8,16,16,32]{4,3,2,1,0:T(8,128)S(1)} %reshape.434, s32[16,32]{1,0:T(8,128)S(1)} %multiply_add_fusion), kind=kOutput, calls=%fused_computation.16 | convolution fusion | flops 809238528 | bytes 1050624 | tf_op jit(solution)/shard_map/lkpqxb,qbm->lkpxm/dot_general | solution.py:63
  69.8 6.4 %convolution_bitcast_fusion.6 = f32[2,8,16,512]{3,2,1,0:T(8,128)S(1)} fusion(f32[2,8,16,16,32]{4,3,2,1,0:T(8,128)S(1)} %copy-done, s32[16,32]{1,0:T(8,128)S(1)} %multiply_add_fusion), kind=kOutput, calls=%fused_computation.19 | convolution fusion | flops 809238528 | bytes 1050624 | tf_op jit(solution)/shard_map/lkpqxb,qbm->lkpxm/dot_general | solution.py:61
  76.2 6.0 %fusion.7 = f32[2,8,16,512]{3,2,1,0:T(8,128)S(1)} fusion(f32[2,8,16,512]{3,2,1,0:T(8,128)S(1)} %convolution_bitcast_fusion.3, f32[2,8,16,16,32]{4,3,2,1,0:T(8,128)S(1)} %copy-done, s32[16,32]{1,0:T(8,128)S(1)} %multiply_add_fusion), kind=kOutput, calls=%fused_computation.34 | convolution fusion | flops 809107456 | bytes 1574912 | tf_op jit(solution)/shard_map/lkpqxb,qbm->lkpxm/dot_general | solution.py:62
  82.2 6.1 %fusion.6 = f32[2,8,16,512]{3,2,1,0:T(8,128)S(1)} fusion(f32[2,8,16,512]{3,2,1,0:T(8,128)S(1)} %convolution_bitcast_fusion.6, f32[2,8,16,16,32]{4,3,2,1,0:T(8,128)S(1)} %reshape.434, s32[16,32]{1,0:T(8,128)S(1)} %multiply_add_fusion), kind=kOutput, calls=%fused_computation.33 | convolution fusion | flops 809107456 | bytes 1574912 | tf_op jit(solution)/shard_map/lkpqxb,qbm->lkpxm/dot_general | solution.py:60
  94.0 2.5 copy.75
  101.8 7.1 %fusion.21 = f32[16,32,2,8,16]{1,4,3,2,0:T(8,128)S(1)} fusion(s32[16,32]{1,0:T(8,128)S(1)} %multiply_add_fusion, f32[2,8,16,512]{3,2,0,1:T(8,128)S(1)} %fusion.1), kind=kOutput, calls=%fused_computation.51 | convolution fusion | flops 808976384 | bytes 1050624 | tf_op jit(solution)/shard_map/lkpxm,mqb->lkpqxb/dot_general | solution.py:60
  109.8 7.5 %fusion.19 = f32[16,32,2,8,16]{1,4,3,2,0:T(8,128)S(1)} fusion(s32[16,32]{1,0:T(8,128)S(1)} %multiply_add_fusion, f32[2,8,16,512]{3,2,0,1:T(8,128)S(1)} %fusion), kind=kOutput, calls=%fused_computation.49 | convolution fusion | flops 808976384 | bytes 1050624 | tf_op jit(solution)/shard_map/lkpxm,mqb->lkpqxb/dot_general | solution.py:62
  117.3 7.3 %subtract_bitcast_fusion = f32[1,2,8,16,16,32]{5,4,2,1,3,0:T(8,128)S(1)} fusion(f32[16,32,2,8,16]{1,4,3,2,0:T(8,128)S(1)} %fusion.21, s32[16,32]{1,0:T(8,128)S(1)} %multiply_add_fusion, f32[2,8,16,512]{3,2,0,1:T(8,128)S(1)} %fusion), kind=kOutput, calls=%fused_computation.4 | convolution fusion | flops 809107456 | bytes 1574912 | tf_op jit(solution)/shard_map/lkpxm,mqb->lkpqxb/dot_general | solution.py:61
  124.6 7.1 %add_bitcast_fusion = f32[1,2,8,16,16,32]{5,4,2,1,3,0:T(8,128)S(1)} fusion(f32[16,32,2,8,16]{1,4,3,2,0:T(8,128)S(1)} %fusion.19, s32[16,32]{1,0:T(8,128)S(1)} %multiply_add_fusion, f32[2,8,16,512]{3,2,0,1:T(8,128)S(1)} %fusion.1), kind=kOutput, calls=%fused_computation.3 | convolution fusion | flops 809107456 | bytes 1574912 | tf_op jit(solution)/shard_map/lkpxm,mqb->lkpqxb/dot_general | solution.py:63
  134.8 3.5 %reshape_reshape.4 = f32[2,2,128,512]{3,2,1,0:T(8,128)S(1)} reshape(f32[2,2,8,16,16,32]{5,4,3,2,1,0:T(8,128)} %copy.80) | data formatting | bytes 2097152 | tf_op jit(solution)/shard_map/reshape;reshape | solution.py:16
  139.2 5.5 %all_to_all.25 = f32[64,2,2,2,512]{4,0,3,2,1:T(8,128)S(1)} all-to-all(f32[64,2,2,2,512]{4,0,3,2,1:T(8,128)S(1)} %copy.81), channel_id=1, replica_groups=mesh['px_0'=2,'px_1'=4,'py_0'=4,'py_1'=2,'py_2'=2] {'py_2'}, dimensions={1} | all-to-all | bytes 2097152 | tf_op jit(solution)/shard_map/all_to_all | solution.py:29
  145.5 22.0 %all_to_all.26 = f32[64,2,2,2,512]{4,1,3,2,0:T(2,128)S(1)} all-to-all(f32[64,2,2,2,512]{4,1,3,2,0:T(2,128)S(1)} %copy.82), channel_id=1, replica_groups=mesh['px_0'=2,'px_1'=4,'py_0'=4,'py_1'=2,'py_2'=2] {'px_0','px_1','py_0'..., dimensions={0} | all-to-all | bytes 2097152 | tf_op jit(solution)/shard_map/all_to_all | solution.py:29
  176.0 2.6 convolution_subtract_fusion.1
  178.6 34.9 %concatenate.36 = f32[1,8,2,16,2,128,2]{6,5,4,3,2,1,0:T(8,128)} reshape(f32[16,32,256]{2,1,0:T(8,128)S(1)} %convolution_subtract_fusion.1) | data formatting | bytes 1048576 | tf_op jit(solution)/shard_map/concatenate | solution.py:64
  213.5 19.7 %copy.88 = f32[1,8,2,16,2,128,2]{5,3,6,4,2,1,0:T(8,128)S(1)} copy(f32[1,8,2,16,2,128,2]{6,5,4,3,2,1,0:T(8,128)} %concatenate.36) | data formatting | bytes 1048576 | tf_op jit(solution)/shard_map/concatenate | solution.py:64
  234.7 34.9 %concatenate.37 = f32[1,8,2,16,2,128,2]{6,5,4,3,2,1,0:T(8,128)} reshape(f32[16,32,256]{2,1,0:T(8,128)S(1)} %convolution_add_fusion.1) | data formatting | bytes 1048576 | tf_op jit(solution)/shard_map/concatenate | solution.py:64
  269.6 19.4 %copy.89 = f32[1,8,2,16,2,128,2]{5,3,6,4,2,1,0:T(8,128)S(1)} copy(f32[1,8,2,16,2,128,2]{6,5,4,3,2,1,0:T(8,128)} %concatenate.37) | data formatting | bytes 1048576 | tf_op jit(solution)/shard_map/concatenate | solution.py:64
  289.2 9.7 %div.31 = f32[2,4,2,8,2,64,2]{6,5,4,3,2,1,0:T(8,128)} reshape(f32[2,8,16,128]{3,2,1,0:T(8,128)S(1)} %broadcast_multiply_fusion) | data formatting | bytes 262144 | tf_op jit(solution)/shard_map/div | solution.py:128
  298.9 4.0 %reduce_sum.28 = f32[2,4,8,64]{3,2,1,0:T(8,128)S(1)} reduce(f32[2,4,2,8,2,64,2]{6,5,4,3,2,1,0:T(8,128)} %div.31, f32[]{:T(128)} %constant.105.clone.1), dimensions={2,4,6}, to_apply=%region_1.2 | reduce | flops 28672 | bytes 147460 | tf_op jit(solution)/shard_map/reduce_sum | solution.py:128
  308.9 29.5 %all-gather.4.cloned.1.call-done = f32[16,1,37376]{2,1,0:T(1,128)} async-done(((f32[1,1,37376]{2,1,0:T(1,128)}), f32[16,1,37376]{2,1,0:T(1,128)}) %all-gather.4.cloned.1.call-update) | async-done | bytes 2392080 | tf_op jit(solution)/shard_map/all_gather | solution.py:41
  (72 shorter events, 45.7 us)
Async XLA Ops:
  7.2 5.4 %copy-start.1 = (f32[2,16,32,256]{3,2,1,0:T(8,128)S(1)}, f32[2,16,32,256]{3,2,1,0:T(8,128)}, u32[]{:S(2)}) copy-start(f32[2,16,32,256]{3,2,1,0:T(8,128)} %param.3) | copy-start | bytes 3145732
  9.9 5.9 %copy-start.2 = (f32[16,32,256]{2,1,0:T(8,128)S(1)}, f32[16,32,256]{2,1,0:T(8,128)}, u32[]{:S(2)}) copy-start(f32[16,32,256]{2,1,0:T(8,128)} %param.4) | copy-start | bytes 1572868
  17.9 41.2 %all-to-all-start = ((f32[3,256,512]{2,0,1:T(4,128)}), f32[3,256,512]{2,0,1:T(4,128)S(1)}, u32[]{:S(2)}, u32[]{:S(2)}) async-start(f32[3,256,512]{2,0,1:T(4,128)} %copy.71), calls=%async_computation | async-start | bytes 4194304 | tf_op jit(solution)/shard_map/all_to_all | solution.py:79
  29.4 309.0 %all-gather.4.cloned.1.call-start = ((), (), s32[]{:S(2)}) async-start(), calls=%async_computation.3 | async-start | bytes 2541568 | tf_op jit(solution)/shard_map/all_gather | solution.py:41
  63.8 6.0 %copy-start = (f32[2,8,16,16,32]{4,3,2,1,0:T(8,128)S(1)}, f32[2,8,16,16,32]{4,3,2,1,0:T(8,128)}, u32[]{:S(2)}) copy-start(f32[2,8,16,16,32]{4,3,2,1,0:T(8,128)} %reshape.435) | copy-start | bytes 1572868
  302.9 2.3 copy-start.3
Sparse Core Ops, SparseCore 0:
  305.3 33.0 all-gather.3
where the time goes:
time: 357 us; the launch traced here: 351 us
  local copies, waits for them, and re-layouts  152 us (43%)
  matrix products  77.3 us (22%)
  waiting for transfers between devices  58.9 us (16%)
  blocking collectives  27.5 us (8%)
  between operations  16.9 us (5%)
  starting transfers between devices  11.7 us (3%)
  other arithmetic  6.3 us (2%)
    concatenate x5, local copies, waits for them, and re-layouts, complex_apply(): return jnp.concatenate([real_cos - imag_sin, imag_cos + real_sin], 0)  111 us
    all_gather x1, waiting for transfers between devices, gather_together(): lines, at, gathered = (lax.all_gather(line, axis), 0, [])  29.5 us
    all_to_all x1, waiting for transfers between devices, forward(): lax.all_to_all(flat, PX_PY, split_axis=1, concat_axis=2, tiled=True)  29.4 us
    all_to_all x2, blocking collectives, moved_by_axis(): whole = lax.all_to_all(whole, axes[k], k, k, tiled=True)  27.5 us
    dot_general x6, matrix products, complex_apply(): jnp.einsum(pattern, real_part, table_cos, precision=lax.Precision.HIGHEST)  20 us
    dot_general x6, matrix products, complex_apply(): jnp.einsum(pattern, imag_part, table_sin, precision=lax.Precision.HIGHEST)  19.7 us
    dot_general x6, matrix products, complex_apply(): jnp.einsum(pattern, imag_part, table_cos, precision=lax.Precision.HIGHEST)  19.5 us
    dot_general x6, matrix products, complex_apply(): jnp.einsum(pattern, real_part, table_sin, precision=lax.Precision.HIGHEST)  18 us
  transfers between devices with their start and end apart: 2, of which 2 were waited for; matrix products, arithmetic and copies ran while one was open for 0% of the time, Pallas kernels for 0%

commit v1 on v0

v1 whole, which is shorter than its diff:
```python
import functools

import jax
import jax.numpy as jnp
import ml_dtypes
import numpy as np
from jax import lax
from jax.experimental import pallas as pl
from jax.experimental.pallas import tpu as pltpu
from jax.sharding import Mesh
from jax.sharding import PartitionSpec as P

PX = ("px_0", "px_1")
PY = ("py_0", "py_1", "py_2")
F32 = jnp.float32
BF16 = jnp.bfloat16
LOGICAL = pl.DeviceIdType.LOGICAL

NX, NY, NZ = 128, 512, 256
CX, CY = 16, 32
CELLS = CX * CY
T_Z, T_P, T_C, T_CI, T_PI, T_U, TABLES = 0, 1, 2, 6, 10, 11, 12
PIECE = 24


def wave(products, length, sign):
    angles = 2.0 * np.pi * (products % length) / length
    return np.cos(angles), sign * np.sin(angles)


def applied_left(real, imag):
    return np.block([[real, -imag], [imag, real]])


def build_tables():
    spots = np.arange(128)
    z = np.arange(NZ)
    p, q = spots // 16, spots % 16
    j1, m1 = spots // 16, spots % 16
    tables = np.zeros((TABLES, 256, 256))
    cos_z, sin_z = wave(spots[:, None] * z[None, :], NZ, -1.0)
    sin_z[0] = (-1.0) ** z
    tables[T_Z] = np.concatenate([cos_z, sin_z], 0)
    weight = np.where(spots == 0, 1.0, 2.0)[:, None] / float(NX * NY * NZ)
    tables[T_U] = np.concatenate([cos_z * weight, sin_z * weight], 0)
    outer = 2 * p[None, :] * j1[:, None] + q[None, :] * m1[:, None]
    tables[T_P] = applied_left(*wave(outer, 16, -1.0))
    tables[T_PI] = applied_left(*wave(outer.T, 16, 1.0))
    low, b = spots // 32, spots % 32
    half, j2b, q2 = spots // 64, (spots // 16) % 4, spots % 16
    m2 = 2 * q2 + half
    for j2a in range(4):
        inner = 2 * low[:, None] * j2a + 8 * low[:, None] * j2b[None, :] + b[:, None] * m2[None, :]
        tables[T_C + j2a] = applied_left(*wave(inner.T, 32, -1.0)).T
        tables[T_CI + j2a] = applied_left(*wave(inner, 32, 1.0)).T
    cell_a, cell_b = np.arange(CELLS) // CY, np.arange(CELLS) % CY
    middle = 4 * cell_a[None, :] * j1[:, None] + cell_b[None, :] * m1[:, None]
    twiddle = np.stack(wave(middle, 512, -1.0)).astype(np.float32)
    high = tables.astype(np.float32).astype(ml_dtypes.bfloat16)
    rest = (tables - high.astype(np.float64)).astype(np.float32).astype(ml_dtypes.bfloat16)
    pairs = np.zeros((NZ, 256))
    pairs[z, z // 2] = 0.5
    pairs[z, 128 + z // 4] = 0.25
    pairs[z, 192 + z // 8] = 0.125
    rows = np.zeros((8 * PIECE, CELLS))
    for cell in range(CELLS):
        a, b = divmod(cell, CY)
        rows[(a // 2) * PIECE + b // 2, cell] = 0.25
        second = (a // 4) * 8 + b // 4
        rows[(second // 4) * PIECE + 16 + second % 4, cell] = 1.0 / 16
        third = (a // 8) * 4 + b // 8
        rows[third * PIECE + 20, cell] = 1.0 / 64
    exact = ml_dtypes.bfloat16
    return np.stack([high, rest], 1), twiddle, pairs.astype(exact), rows.astype(exact)


def dot(left, right):
    return jnp.dot(left, right, preferred_element_type=F32)


def dot_nt(left, right):
    return lax.dot_general(left, right, (((1,), (1,)), ((), ())), preferred_element_type=F32)


def split(values):
    high = values.astype(BF16)
    return high, (values - high.astype(F32)).astype(BF16)


def ordered(index):
    return lax.rem(2 - index + 3 * (index // 2) + 2 * (index // 3) + 4, 4)


def kernel(
    noise_hbm, spec_hbm, order_ref, tables_hbm, twiddle_hbm, pairs_hbm, rows_hbm,
    modulus_ref, one_ref, two_ref, three_ref,
    noise, spec, tables, twiddle, pairs, rows,
    s_send, s_recv, n_send, scale, f_send, f_recv, b_send, b_recv,
    y_mid, v_high, v_low, v_back, z_high, z_low, g_high, g_low,
    r_send, r_recv, t_send, t_recv,
    load_sems, send_sems, recv_sems,
):
    zh, y, x, zl, c = [lax.axis_index(a) for a in (*PX, *PY)]
    z = zh * 2 + zl
    line = zh * 64 + y * 16
    column = x * 4 + zl * 2 + c
    me = line + column

    loads = []
    for k, (source, target) in enumerate((
        (spec_hbm, spec), (tables_hbm.at[T_Z], tables.at[T_Z]), (noise_hbm, noise),
        (tables_hbm.at[pl.ds(1, TABLES - 1)], tables.at[pl.ds(1, TABLES - 1)]),
        (twiddle_hbm, twiddle), (pairs_hbm, pairs), (rows_hbm, rows),
    )):
        load = pltpu.make_async_copy(source, target, load_sems.at[k])
        load.start()
        loads.append(load)

    def over_devices(action):
        def group(n, skip):
            core = lax.rem(c + 1 - n // 4, 2)
            s = lax.rem(n, 4)
            z2 = lax.rem(z + ordered(s), 4)
            base = (z2 // 2) * 64 + lax.rem(z2, 2) * 2 + core
            ys = [base + lax.rem(y + ordered(lax.rem(s + t, 4)), 4) * 16 for t in range(4)]
            xs = [lax.rem(x + ordered(lax.rem(s + t, 4)), 4) * 4 for t in range(4)]
            for t in range(4):
                for u in range(4):
                    if not (skip and t == 0 and u == 0):
                        action(ys[t] + xs[u])

        @pl.loop(0, 7)
        def _(n):
            group(n, False)

        group(jnp.int32(7), True)

    barrier = pltpu.get_barrier_semaphore()
    over_devices(lambda d: pl.semaphore_signal(barrier, 1, device_id=d, device_id_type=LOGICAL))

    def send_all(source, target, index):
        over_devices(lambda d: pltpu.make_async_remote_copy(
            source(d), target(me), send_sems.at[index], recv_sems.at[index],
            device_id=d, device_id_type=LOGICAL).start())

    def finish(ref, sem):
        pltpu.make_async_copy(ref, ref, sem).wait()

    loads[0].wait()
    for jj in range(4):
        j2lo, m2lo = divmod(jj, 2)
        starts = [(j2lo * 8 + j1) * CY + m2lo * 16 for j1 in range(8)]
        block = jnp.concatenate([spec[pl.ds(s, 16), 0:128] for s in starts], 0)
        s_send[:, jj, :] = block.T
        block = jnp.concatenate([spec[pl.ds(s, 16), 128:256] for s in starts], 0)
        n_send[0, jj, :] = block.T[0]

    pl.semaphore_wait(barrier, 127)
    send_all(lambda d: s_send.at[d], lambda m: s_recv.at[0, m], 0)
    s_recv[0, me] = s_send[me]

    @pl.when(me != 0)
    def _():
        pltpu.make_async_remote_copy(
            n_send.at[0], s_recv.at[1, me], send_sems.at[1], recv_sems.at[1],
            device_id=jnp.int32(0), device_id_type=LOGICAL).start()

    @pl.when(me == 0)
    def _():
        s_recv[1, 0] = n_send[0]

    loads[1].wait()
    loads[2].wait()

    @pl.loop(0, 2)
    def _(f):
        for part in range(2):
            high, low = split(noise[f, pl.ds(part * 256, 256), :])
            out = dot_nt(tables[T_Z, 0], high) + dot_nt(tables[T_Z, 0], low) + dot_nt(tables[T_Z, 1], high)
            for ri in range(2):
                for l in range(2):
                    f_send[f, pl.ds(ri * 4 + part * 2 + l, 128, stride=8), :] = (
                        out[ri * 128:(ri + 1) * 128, l * 128:(l + 1) * 128])

    def swap_first(ref):
        first, second = ref[0, pl.ds(0, 8), :], ref[1, pl.ds(0, 8), :]
        ref[0, pl.ds(0, 8), :] = jnp.concatenate([first[:4], second[:4]], 0)
        ref[1, pl.ds(0, 8), :] = jnp.concatenate([first[4:], second[4:]], 0)

    def block_of(d):
        return pl.ds(pl.multiple_of(d * 8, 8), 8)

    swap_first(f_send)

    @pl.loop(0, 2)
    def _(f):
        send_all(lambda d: f_send.at[f, block_of(d)], lambda m: f_recv.at[f, block_of(m)], 2 + f)
        f_recv[f, block_of(me), :] = f_send[f, block_of(me), :]

    finish(s_recv.at[0, pl.ds(0, 127)], recv_sems.at[0])

    @pl.when(me == 0)
    def _():
        finish(s_recv.at[0, pl.ds(0, 127)], recv_sems.at[1])

    for plane in range(2):
        slot = jnp.where(me == 0, plane, 0)
        for j2a in range(4):
            parts = []
            for m2lo in range(2):
                for p_high in range(4):
                    first = p_high * 32 + (j2a // 2) * 16
                    parts.append(s_recv[slot, pl.ds(first, 16), (j2a % 2) * 2 + m2lo, :])
            scale[plane, j2a] = jnp.concatenate(parts, 0).T

    for load in loads[3:]:
        load.wait()

    @pl.loop(0, 2)
    def _(f):
        finish(f_recv.at[f, pl.ds(0, 127 * 8)], recv_sems.at[2 + f])
        for part in range(2):
            values = jnp.concatenate([
                jnp.concatenate([
                    f_recv[f, pl.ds(ri * 4 + part * 2 + l, 128, stride=8), :] for l in range(2)], 1)
                for ri in range(2)], 0)
            high, low = split(values)
            y_mid[:, part * 256:(part + 1) * 256] = (
                dot(tables[T_P, 0], high) + dot(tables[T_P, 0], low) + dot(tables[T_P, 1], high))

        @pl.loop(0, 8)
        def _(n):
            at = pl.multiple_of(n * 16, 16)
            real, imag = [], []
            for l in range(4):
                lanes = slice(l * 128, (l + 1) * 128)
                vr, vi = y_mid[pl.ds(at, 16), lanes], y_mid[pl.ds(128 + at, 16), lanes]
                wr, wi = twiddle[0, pl.ds(at, 16), lanes], twiddle[1, pl.ds(at, 16), lanes]
                real.append(vr * wr - vi * wi)
                imag.append(vr * wi + vi * wr)
            r02, r13 = real[0] + real[2], real[1] + real[3]
            i02, i13 = imag[0] + imag[2], imag[1] + imag[3]
            rd, re = real[0] - real[2], real[1] - real[3]
            id_, ie = imag[0] - imag[2], imag[1] - imag[3]
            outs = ((r02 + r13, i02 + i13), (rd + ie, id_ - re), (r02 - r13, i02 - i13), (rd - ie, id_ + re))
            for j2a, pair in enumerate(outs):
                for ri in range(2):
                    high, low = split(pair[ri])
                    v_high[j2a, pl.ds(at, 16), ri * 128:(ri + 1) * 128] = high
                    v_low[j2a, pl.ds(at, 16), ri * 128:(ri + 1) * 128] = low

        for j2a in range(4):
            high, low = v_high[j2a], v_low[j2a]
            spectral = (dot(high, tables[T_C + j2a, 0]) + dot(low, tables[T_C + j2a, 0])
                        + dot(high, tables[T_C + j2a, 1]))
            factor = scale[f, j2a]
            high, low = split(spectral * jnp.concatenate([factor, factor], 1))
            v_back[j2a] = (dot(high, tables[T_CI + j2a, 0]) + dot(low, tables[T_CI + j2a, 0])
                           + dot(high, tables[T_CI + j2a, 1]))

        @pl.loop(0, 8)
        def _(n):
            at = pl.multiple_of(n * 16, 16)
            real = [v_back[j2a, pl.ds(at, 16), 0:128] for j2a in range(4)]
            imag = [v_back[j2a, pl.ds(at, 16), 128:256] for j2a in range(4)]
            r02, r13 = real[0] + real[2], real[1] + real[3]
            i02, i13 = imag[0] + imag[2], imag[1] + imag[3]
            rd, re = real[0] - real[2], real[1] - real[3]
            id_, ie = imag[0] - imag[2], imag[1] - imag[3]
            outs = ((r02 + r13, i02 + i13), (rd - ie, id_ + re), (r02 - r13, i02 - i13), (rd + ie, id_ - re))
            for l, (vr, vi) in enumerate(outs):
                lanes = slice(l * 128, (l + 1) * 128)
                wr, wi = twiddle[0, pl.ds(at, 16), lanes], twiddle[1, pl.ds(at, 16), lanes]
                for ri, value in enumerate((vr * wr + vi * wi, vi * wr - vr * wi)):
                    high, low = split(value)
                    z_high[pl.ds(ri * 128 + at, 16), lanes] = high
                    z_low[pl.ds(ri * 128 + at, 16), lanes] = low

        for part in range(2):
            high, low = z_high[:, part * 256:(part + 1) * 256], z_low[:, part * 256:(part + 1) * 256]
            out = dot(tables[T_PI, 0], high) + dot(tables[T_PI, 0], low) + dot(tables[T_PI, 1], high)
            for ri in range(2):
                for l in range(2):
                    b_send[f, pl.ds(ri * 4 + part * 2 + l, 128, stride=8), :] = (
                        out[ri * 128:(ri + 1) * 128, l * 128:(l + 1) * 128])
        send_all(lambda d: b_send.at[f, block_of(d)], lambda m: b_recv.at[f, block_of(m)], 4 + f)
        b_recv[f, block_of(me), :] = b_send[f, block_of(me), :]

    for f in range(2):
        finish(b_recv.at[f, pl.ds(0, 127 * 8)], recv_sems.at[4 + f])
    swap_first(b_recv)

    def over_column(action):
        for dx in (2, 1, 3, 0):
            for dz in (1, 0):
                for dc in (1, 0):
                    if (dx, dz, dc) != (0, 0, 0):
                        action(lax.rem(x + dx, 4) * 4 + lax.rem(zl + dz, 2) * 2 + lax.rem(c + dc, 2))

    @pl.loop(0, 2)
    def _(f):
        for l in range(4):
            cells = pl.ds(l * 128, 128)
            values = jnp.concatenate(
                [b_recv[f, pl.ds(ri * 4 + l, 128, stride=8), :].T for ri in range(2)], 1)
            high, low = split(values)
            fields = dot(high, tables[T_U, 0]) + dot(low, tables[T_U, 0]) + dot(high, tables[T_U, 1])
            modulus = jnp.exp(0.5 * fields)
            modulus_ref[f, cells, :] = modulus
            high, low = split(modulus)
            high, low = split(dot(high, pairs[...]) + dot(low, pairs[...]))
            g_high[cells, :] = high
            g_low[cells, :] = low
        coarse = dot(rows[...], g_high[...]) + dot(rows[...], g_low[...])
        for i in range(8):
            r_send[f * 8 + i, pl.ds(0, 16), :] = coarse[i * PIECE:i * PIECE + 16, 0:128]
            r_send[f * 8 + i, pl.ds(16, 8), :] = coarse[i * PIECE + 16:(i + 1) * PIECE, 128:256]

    over_column(lambda g: pltpu.make_async_remote_copy(
        r_send.at[g], r_recv.at[column], send_sems.at[6], recv_sems.at[6],
        device_id=line + g, device_id_type=LOGICAL).start())
    r_recv[column] = r_send[column]
    finish(r_recv.at[pl.ds(0, 15)], recv_sems.at[6])

    lower = lax.broadcasted_iota(jnp.int32, (8, 128), 0) < 4

    @pl.loop(0, 16)
    def _(g):
        t_send[g, pl.ds(0, 16), :] = r_recv[order_ref[0, g], pl.ds(0, 16), :]
        second = r_recv[order_ref[1, g], pl.ds(16, 8), :]
        third = r_recv[order_ref[2, g], pl.ds(16, 8), :]
        t_send[g, pl.ds(16, 8), :] = jnp.where(lower, second, third)

    over_column(lambda g: pltpu.make_async_remote_copy(
        t_send.at[g], t_recv.at[column], send_sems.at[7], recv_sems.at[7],
        device_id=line + g, device_id_type=LOGICAL).start())
    t_recv[column] = t_send[column]
    finish(t_recv.at[pl.ds(0, 15)], recv_sems.at[7])
    for i in range(16):
        one_ref[pl.ds(i * 16, 16), :] = t_recv[i, pl.ds(0, 16), :]
        tail = t_recv[i, pl.ds(16, 8), :]
        two_ref[pl.ds(i * 4, 4), :] = tail[0:4, 0:64]
        three_ref[pl.ds(i, 1), :] = tail[4:5, 64:96]

    finish(s_send.at[pl.ds(0, 127)], send_sems.at[0])

    @pl.when(me != 0)
    def _():
        finish(n_send.at[0], send_sems.at[1])

    for f in range(2):
        finish(f_send.at[f, pl.ds(0, 127 * 8)], send_sems.at[2 + f])
        finish(b_send.at[f, pl.ds(0, 127 * 8)], send_sems.at[4 + f])
    finish(r_send.at[pl.ds(0, 15)], send_sems.at[6])
    finish(t_send.at[pl.ds(0, 15)], send_sems.at[7])


def on_device(white_noise, spectrum, group_table):
    tables, twiddle, pairs, rows = build_tables()
    anywhere = pl.BlockSpec(memory_space=pl.ANY)
    vmem = pl.BlockSpec(memory_space=pltpu.VMEM)
    modulus, one, two, three = pl.pallas_call(
        kernel,
        out_shape=(
            jax.ShapeDtypeStruct((2, CELLS, NZ), F32),
            jax.ShapeDtypeStruct((256, 128), F32),
            jax.ShapeDtypeStruct((64, 64), F32),
            jax.ShapeDtypeStruct((16, 32), F32),
        ),
        in_specs=[anywhere, anywhere, pl.BlockSpec(memory_space=pltpu.SMEM)] + [anywhere] * 4,
        out_specs=(vmem, vmem, vmem, vmem),
        scratch_shapes=[
            pltpu.VMEM((2, CELLS, NZ), F32),
            pltpu.VMEM((CELLS, NZ), F32),
            pltpu.VMEM((TABLES, 2, 256, 256), BF16),
            pltpu.VMEM((2, 128, CELLS), F32),
            pltpu.VMEM((NZ, 256), BF16),
            pltpu.VMEM((8 * PIECE, CELLS), BF16),
            pltpu.VMEM((128, 4, 128), F32),
            pltpu.VMEM((2, 128, 4, 128), F32),
            pltpu.VMEM((1, 4, 128), F32),
            pltpu.VMEM((2, 4, 128, 128), F32),
            pltpu.VMEM((2, 1024, 128), F32),
            pltpu.VMEM((2, 1024, 128), F32),
            pltpu.VMEM((2, 1024, 128), F32),
            pltpu.VMEM((2, 1024, 128), F32),
            pltpu.VMEM((256, CELLS), F32),
            pltpu.VMEM((4, 128, 256), BF16),
            pltpu.VMEM((4, 128, 256), BF16),
            pltpu.VMEM((4, 128, 256), F32),
            pltpu.VMEM((256, CELLS), BF16),
            pltpu.VMEM((256, CELLS), BF16),
            pltpu.VMEM((CELLS, 256), BF16),
            pltpu.VMEM((CELLS, 256), BF16),
            pltpu.VMEM((16, PIECE, 128), F32),
            pltpu.VMEM((16, PIECE, 128), F32),
            pltpu.VMEM((16, PIECE, 128), F32),
            pltpu.VMEM((16, PIECE, 128), F32),
            pltpu.SemaphoreType.DMA((7,)),
            pltpu.SemaphoreType.DMA((8,)),
            pltpu.SemaphoreType.DMA((8,)),
        ],
        compiler_params=pltpu.CompilerParams(
            collective_id=0, has_side_effects=True, vmem_limit_bytes=48 << 20),
        name="moduli",
    )(
        white_noise.reshape(2, CELLS, NZ), spectrum.reshape(CELLS, NZ), group_table,
        jnp.asarray(tables), jnp.asarray(twiddle), jnp.asarray(pairs), jnp.asarray(rows),
    )
    return (
        modulus.reshape(2, CX, CY, NZ),
        one.reshape(2, 8, 16, 128),
        two.reshape(2, 4, 8, 64),
        three.reshape(2, 2, 4, 32),
    )


def solution(mesh):
    split_mesh = Mesh(mesh.devices.reshape(2, 4, 4, 2, 2), (*PX, *PY))
    whole = P(None, PX, PY, None)
    return jax.shard_map(
        on_device,
        mesh=split_mesh,
        in_specs=(whole, P(PX, PY, None), P()),
        out_specs=(whole, whole, whole, whole),
        check_vma=False,
    )
```

time: 357 us -> 66.5 us (0.19); the launches traced: 351 us -> 66.2 us
  local copies, waits for them, and re-layouts: 152 us -> 8.65 us
  matrix products: 77.3 us -> 0 us
  waiting for transfers between devices: 58.9 us -> 0 us
  Pallas kernels: 0 us -> 56.9 us
  blocking collectives: 27.5 us -> 0 us
  between operations: 16.9 us -> 0.65 us
  starting transfers between devices: 11.7 us -> 0 us
  other arithmetic: 6.3 us -> 0 us
    concatenate x6 -> x0, local copies, waits for them, and re-layouts: 113 us -> none  [the longest x5 111 us: complex_apply(): return jnp.concatenate([real_cos - imag_sin, imag_cos + real_sin], 0)]
    dot_general x24 -> x0, matrix products: 77.3 us -> none  [the longest x6 20 us: complex_apply(): jnp.einsum(pattern, real_part, table_cos, precision=lax.Precision.HIGHEST)]
    pallas_call x0 -> x1, Pallas kernels: none -> 56.9 us  [on_device(): pl.pallas_call(kernel, out_shape=(jax.ShapeDtypeStruct((2, CELLS, NZ), F3...]
    all_gather x1 -> x0, waiting for transfers between devices: 29.5 us -> none  [gather_together(): lines, at, gathered = (lax.all_gather(line, axis), 0, [])]
    all_to_all x1 -> x0, waiting for transfers between devices: 29.4 us -> none  [forward(): lax.all_to_all(flat, PX_PY, split_axis=1, concat_axis=2, tiled=True)]
    all_to_all x2 -> x0, blocking collectives: 27.5 us -> none  [moved_by_axis(): whole = lax.all_to_all(whole, axes[k], k, k, tiled=True)]
    all_to_all x1 -> x0, starting transfers between devices: 11.5 us -> none  [forward(): lax.all_to_all(flat, PX_PY, split_axis=1, concat_axis=2, tiled=True)]
    div x4 -> x0, local copies, waits for them, and re-layouts: 11 us -> none  [coarsen(): return blocks.mean(axis=(2, 4, 6))]
  transfers between devices with their start and end apart: 2 -> 0, of which waited for: 2 -> 0; matrix products, arithmetic and copies ran while one was open for 0% -> 0% of each run, Pallas kernels for 0% -> 0%
where the time goes in v1:
time: 66.5 us; the launch traced here: 66.2 us
  Pallas kernels  56.9 us (86%)
  local copies, waits for them, and re-layouts  8.65 us (13%)
    pallas_call x1, Pallas kernels, on_device(): pl.pallas_call(kernel, out_shape=(jax.ShapeDtypeStruct((2, CELLS, NZ), F3...  56.9 us
    unnamed x16, local copies, waits for them, and re-layouts  8.65 us

profile of v1, /device:TPU:1, one launch (start us, length us, event | category | flops | bytes accessed | tf_op | source)
XLA Modules:
  0.0 66.2 jit_solution(17175892154426304820)
XLA Ops:
  0.6 0.0 copy-start
  0.6 1.2 %copy-done = f32[2,16,32,256]{3,2,1,0:T(8,128)S(1)} copy-done((f32[2,16,32,256]{3,2,1,0:T(8,128)S(1)}, f32[2,16,32,256]{3,2,1,0:T(8,128)}, u32[]{:S(2)}) %copy-start) | copy-done | bytes 1048600
  1.9 0.0 copy-start.1
  1.9 1.0 %copy-done.1 = f32[16,32,256]{2,1,0:T(8,128)S(1)} copy-done((f32[16,32,256]{2,1,0:T(8,128)S(1)}, f32[16,32,256]{2,1,0:T(8,128)}, u32[]{:S(2)}) %copy-start.1) | copy-done | bytes 524312
  2.9 0.0 copy-start.2
  2.9 1.0 %copy-done.2 = f32[2,128,512]{2,1,0:T(8,128)S(1)} copy-done((f32[2,128,512]{2,1,0:T(8,128)S(1)}, f32[2,128,512]{2,1,0:T(8,128)}, u32[]{:S(2)}) %copy-start.2) | copy-done | bytes 524312
  3.9 0.0 copy-start.3
  3.9 0.9 %copy-done.3 = bf16[192,512]{1,0:T(8,128)(2,1)S(1)} copy-done((bf16[192,512]{1,0:T(8,128)(2,1)S(1)}, bf16[192,512]{1,0:T(8,128)(2,1)}, u32[]{:S(2)}) %copy-start.3) | copy-done | bytes 196632
  4.9 0.0 copy-start.4
  4.9 0.9 %copy-done.4 = bf16[256,256]{1,0:T(8,128)(2,1)S(1)} copy-done((bf16[256,256]{1,0:T(8,128)(2,1)S(1)}, bf16[256,256]{1,0:T(8,128)(2,1)}, u32[]{:S(2)}) %copy-start.4) | copy-done | bytes 131096
  5.8 0.0 copy-start.5
  5.8 0.7 %copy-done.5 = s32[3,16]{1,0:T(4,128)S(1)} copy-done((s32[3,16]{1,0:T(4,128)S(1)}, s32[3,16]{1,0:T(4,128)}, u32[]{:S(2)}) %copy-start.5) | copy-done | bytes 216
  6.5 56.9 %moduli.1 = (f32[2,512,256]{2,1,0:T(8,128)S(1)}, f32[256,128]{1,0:T(8,128)S(1)}, f32[64,64]{1,0:T(8,128)S(1)}, f32[16,32]{1,0:T(8,128)S(1)}) custom-call(f32[2,512,256]{2,1,0:T(8,128)S(1)} %bitcast.6, f32[512,256]{1,0:T(8,128)S(1)} %bitcast.8, s32[3,16]{1,0:T(4,128)S(1)} %copy-done.5, bf16[12,2,256,256]{3,2,1,0:T(8,128)(2,1)} %constant.8.clone.tables_hbm, ...), custom_call_target="tpu_custom_call" | custom-call | tf_op jit(solution)/shard_map/moduli/pallas_call | solution.py:362
  63.3 1.0 %copy.15 = f32[2,16,32,256]{3,2,1,0:T(8,128)} copy(f32[2,16,32,256]{3,2,1,0:T(8,128)S(1)} %bitcast.7) | data formatting | bytes 2097152
  64.3 0.7 copy.16
  65.0 0.6 copy.17
  65.6 0.6 copy.18
Async XLA Ops:
  0.6 1.2 %copy-start = (f32[2,16,32,256]{3,2,1,0:T(8,128)S(1)}, f32[2,16,32,256]{3,2,1,0:T(8,128)}, u32[]{:S(2)}) copy-start(f32[2,16,32,256]{3,2,1,0:T(8,128)} %param.7) | copy-start | bytes 3145732
  1.9 1.0 %copy-start.1 = (f32[16,32,256]{2,1,0:T(8,128)S(1)}, f32[16,32,256]{2,1,0:T(8,128)}, u32[]{:S(2)}) copy-start(f32[16,32,256]{2,1,0:T(8,128)} %param.8) | copy-start | bytes 1572868
  2.9 1.0 %copy-start.2 = (f32[2,128,512]{2,1,0:T(8,128)S(1)}, f32[2,128,512]{2,1,0:T(8,128)}, u32[]{:S(2)}) copy-start(f32[2,128,512]{2,1,0:T(8,128)} %constant.9.clone.twiddle_hbm) | copy-start | bytes 1572868
  3.9 0.9 %copy-start.3 = (bf16[192,512]{1,0:T(8,128)(2,1)S(1)}, bf16[192,512]{1,0:T(8,128)(2,1)}, u32[]{:S(2)}) copy-start(bf16[192,512]{1,0:T(8,128)(2,1)} %constant.11.clone.rows_hbm) | copy-start | bytes 589828
  4.9 0.9 %copy-start.4 = (bf16[256,256]{1,0:T(8,128)(2,1)S(1)}, bf16[256,256]{1,0:T(8,128)(2,1)}, u32[]{:S(2)}) copy-start(bf16[256,256]{1,0:T(8,128)(2,1)} %constant.10.clone.pairs_hbm) | copy-start | bytes 393220
  5.8 0.7 %copy-start.5 = (s32[3,16]{1,0:T(4,128)S(1)}, s32[3,16]{1,0:T(4,128)}, u32[]{:S(2)}) copy-start(s32[3,16]{1,0:T(4,128)} %order_ref.1) | copy-start | bytes 580

commit v2 on v1

--- a/solution.py
+++ b/solution.py
@@ -20,7 +20,6 @@
 CX, CY = 16, 32
 CELLS = CX * CY
 T_Z, T_P, T_C, T_CI, T_PI, T_U, TABLES = 0, 1, 2, 6, 10, 11, 12
-PIECE = 24
 
 
 def wave(products, length, sign):
@@ -62,14 +61,12 @@
     pairs[z, z // 2] = 0.5
     pairs[z, 128 + z // 4] = 0.25
     pairs[z, 192 + z // 8] = 0.125
-    rows = np.zeros((8 * PIECE, CELLS))
+    rows = np.zeros((192, CELLS))
     for cell in range(CELLS):
         a, b = divmod(cell, CY)
-        rows[(a // 2) * PIECE + b // 2, cell] = 0.25
-        second = (a // 4) * 8 + b // 4
-        rows[(second // 4) * PIECE + 16 + second % 4, cell] = 1.0 / 16
-        third = (a // 8) * 4 + b // 8
-        rows[third * PIECE + 20, cell] = 1.0 / 64
+        rows[(a // 2) * 16 + b // 2, cell] = 0.25
+        rows[128 + (a // 4) * 8 + b // 4, cell] = 1.0 / 16
+        rows[160 + 2 * ((a // 8) * 4 + b // 8), cell] = 1.0 / 64
     exact = ml_dtypes.bfloat16
     return np.stack([high, rest], 1), twiddle, pairs.astype(exact), rows.astype(exact)
 
@@ -92,13 +89,13 @@
 
 
 def kernel(
-    noise_hbm, spec_hbm, order_ref, tables_hbm, twiddle_hbm, pairs_hbm, rows_hbm,
-    modulus_ref, one_ref, two_ref, three_ref,
-    noise, spec, tables, twiddle, pairs, rows,
+    noise_hbm, spec_hbm, order_hbm, tables_hbm, twiddle_hbm, pairs_hbm, rows_hbm,
+    modulus_ref, fine_ref, rest_ref,
+    order_smem, noise, spec, tables, twiddle, pairs, rows,
     s_send, s_recv, n_send, scale, f_send, f_recv, b_send, b_recv,
     y_mid, v_high, v_low, v_back, z_high, z_low, g_high, g_low,
-    r_send, r_recv, t_send, t_recv,
-    load_sems, send_sems, recv_sems,
+    r_send, r_recv, r_other, r_send_rest, r_recv_rest, r_other_rest, t_send, t_recv, t_send_rest, t_recv_rest,
+    load_sems, send_sems, recv_sems, route_send_sems, route_recv_sems,
 ):
     zh, y, x, zl, c = [lax.axis_index(a) for a in (*PX, *PY)]
     z = zh * 2 + zl
@@ -110,38 +107,42 @@
     for k, (source, target) in enumerate((
         (spec_hbm, spec), (tables_hbm.at[T_Z], tables.at[T_Z]), (noise_hbm, noise),
         (tables_hbm.at[pl.ds(1, TABLES - 1)], tables.at[pl.ds(1, TABLES - 1)]),
-        (twiddle_hbm, twiddle), (pairs_hbm, pairs), (rows_hbm, rows),
+        (twiddle_hbm, twiddle), (pairs_hbm, pairs), (rows_hbm, rows), (order_hbm, order_smem),
     )):
         load = pltpu.make_async_copy(source, target, load_sems.at[k])
         load.start()
         loads.append(load)
 
-    def over_devices(action):
-        def group(n, skip):
-            core = lax.rem(c + 1 - n // 4, 2)
-            s = lax.rem(n, 4)
+    def over_half(action, half):
+        core = lax.rem(c + 1 - half, 2)
+
+        def group(s, skip):
             z2 = lax.rem(z + ordered(s), 4)
             base = (z2 // 2) * 64 + lax.rem(z2, 2) * 2 + core
-            ys = [base + lax.rem(y + ordered(lax.rem(s + t, 4)), 4) * 16 for t in range(4)]
+            ys = [lax.rem(y + ordered(lax.rem(s + t, 4)), 4) * 16 for t in range(4)]
             xs = [lax.rem(x + ordered(lax.rem(s + t, 4)), 4) * 4 for t in range(4)]
             for t in range(4):
                 for u in range(4):
                     if not (skip and t == 0 and u == 0):
-                        action(ys[t] + xs[u])
-
-        @pl.loop(0, 7)
-        def _(n):
-            group(n, False)
-
-        group(jnp.int32(7), True)
+                        action(base + ys[t] + xs[u])
+
+        @pl.loop(0, 4 - half)
+        def _(s):
+            group(s, False)
+
+        if half:
+            group(jnp.int32(3), True)
+
+    def over_devices(action):
+        over_half(action, 0)
+        over_half(action, 1)
 
     barrier = pltpu.get_barrier_semaphore()
     over_devices(lambda d: pl.semaphore_signal(barrier, 1, device_id=d, device_id_type=LOGICAL))
 
-    def send_all(source, target, index):
-        over_devices(lambda d: pltpu.make_async_remote_copy(
-            source(d), target(me), send_sems.at[index], recv_sems.at[index],
-            device_id=d, device_id_type=LOGICAL).start())
+    def send(source, target, send_sem, recv_sem):
+        return lambda d: pltpu.make_async_remote_copy(
+            source(d), target, send_sem, recv_sem, device_id=d, device_id_type=LOGICAL).start()
 
     def finish(ref, sem):
         pltpu.make_async_copy(ref, ref, sem).wait()
@@ -154,20 +155,6 @@
         s_send[:, jj, :] = block.T
         block = jnp.concatenate([spec[pl.ds(s, 16), 128:256] for s in starts], 0)
         n_send[0, jj, :] = block.T[0]
-
-    pl.semaphore_wait(barrier, 127)
-    send_all(lambda d: s_send.at[d], lambda m: s_recv.at[0, m], 0)
-    s_recv[0, me] = s_send[me]
-
-    @pl.when(me != 0)
-    def _():
-        pltpu.make_async_remote_copy(
-            n_send.at[0], s_recv.at[1, me], send_sems.at[1], recv_sems.at[1],
-            device_id=jnp.int32(0), device_id_type=LOGICAL).start()
-
-    @pl.when(me == 0)
-    def _():
-        s_recv[1, 0] = n_send[0]
 
     loads[1].wait()
     loads[2].wait()
@@ -191,34 +178,63 @@
         return pl.ds(pl.multiple_of(d * 8, 8), 8)
 
     swap_first(f_send)
-
-    @pl.loop(0, 2)
-    def _(f):
-        send_all(lambda d: f_send.at[f, block_of(d)], lambda m: f_recv.at[f, block_of(m)], 2 + f)
-        f_recv[f, block_of(me), :] = f_send[f, block_of(me), :]
-
-    finish(s_recv.at[0, pl.ds(0, 127)], recv_sems.at[0])
+    pl.semaphore_wait(barrier, 127)
+    over_devices(send(lambda d: s_send.at[d], s_recv.at[0, me], send_sems.at[0], recv_sems.at[0]))
+    s_recv[0, me] = s_send[me]
 
     @pl.when(me == 0)
     def _():
-        finish(s_recv.at[0, pl.ds(0, 127)], recv_sems.at[1])
-
-    for plane in range(2):
-        slot = jnp.where(me == 0, plane, 0)
+        s_recv[1, 0] = n_send[0]
+
+    def send_forward(f, half):
+        over_half(send(
+            lambda d: f_send.at[f, block_of(d)], f_recv.at[f, block_of(me)],
+            send_sems.at[2 + 2 * f + half], recv_sems.at[2 + f]), half)
+
+    def forward_sent(f, half):
+        finish(f_send.at[f, pl.ds(0, (64 - half) * 8)], send_sems.at[2 + 2 * f + half])
+
+    send_forward(0, 0)
+    send_forward(0, 1)
+    send_forward(1, 0)
+    send_forward(1, 1)
+    @pl.when(me != 0)
+    def _():
+        pltpu.make_async_remote_copy(
+            n_send.at[0], s_recv.at[1, me], send_sems.at[1], recv_sems.at[1],
+            device_id=jnp.int32(0), device_id_type=LOGICAL).start()
+
+    for f in range(2):
+        f_recv[f, block_of(me), :] = f_send[f, block_of(me), :]
+
+    finish(s_recv.at[0, pl.ds(0, 127)], recv_sems.at[0])
+
+    def arrange(plane):
         for j2a in range(4):
             parts = []
             for m2lo in range(2):
                 for p_high in range(4):
                     first = p_high * 32 + (j2a // 2) * 16
-                    parts.append(s_recv[slot, pl.ds(first, 16), (j2a % 2) * 2 + m2lo, :])
+                    parts.append(s_recv[plane, pl.ds(first, 16), (j2a % 2) * 2 + m2lo, :])
             scale[plane, j2a] = jnp.concatenate(parts, 0).T
 
+    arrange(0)
     for load in loads[3:]:
         load.wait()
+
+    def send_back(f):
+        over_devices(send(
+            lambda d: b_send.at[f, block_of(d)], b_recv.at[f, block_of(me)],
+            send_sems.at[6 + f], recv_sems.at[4 + f]))
 
     @pl.loop(0, 2)
     def _(f):
         finish(f_recv.at[f, pl.ds(0, 127 * 8)], recv_sems.at[2 + f])
+        @pl.when(jnp.logical_and(me == 0, f == 1))
+        def _():
+            finish(s_recv.at[1, pl.ds(0, 127)], recv_sems.at[1])
+            arrange(1)
+
         for part in range(2):
             values = jnp.concatenate([
                 jnp.concatenate([
@@ -253,7 +269,7 @@
             high, low = v_high[j2a], v_low[j2a]
             spectral = (dot(high, tables[T_C + j2a, 0]) + dot(low, tables[T_C + j2a, 0])
                         + dot(high, tables[T_C + j2a, 1]))
-            factor = scale[f, j2a]
+            factor = scale[jnp.where(me == 0, f, 0), j2a]
             high, low = split(spectral * jnp.concatenate([factor, factor], 1))
             v_back[j2a] = (dot(high, tables[T_CI + j2a, 0]) + dot(low, tables[T_CI + j2a, 0])
                            + dot(high, tables[T_CI + j2a, 1]))
@@ -281,14 +297,20 @@
             out = dot(tables[T_PI, 0], high) + dot(tables[T_PI, 0], low) + dot(tables[T_PI, 1], high)
             for ri in range(2):
                 for l in range(2):
-                    b_send[f, pl.ds(ri * 4 + part * 2 + l, 128, stride=8), :] = (
+                    half, row = jnp.where(me == 0, ri, f), jnp.where(me == 0, f, ri)
+                    b_send[half, pl.ds(row * 4 + part * 2 + l, 128, stride=8), :] = (
                         out[ri * 128:(ri + 1) * 128, l * 128:(l + 1) * 128])
-        send_all(lambda d: b_send.at[f, block_of(d)], lambda m: b_recv.at[f, block_of(m)], 4 + f)
+
+        @pl.when(jnp.logical_or(me != 0, f == 1))
+        def _():
+            send_back(f)
+
+    @pl.when(me == 0)
+    def _():
+        send_back(0)
+
+    for f in range(2):
         b_recv[f, block_of(me), :] = b_send[f, block_of(me), :]
-
-    for f in range(2):
-        finish(b_recv.at[f, pl.ds(0, 127 * 8)], recv_sems.at[4 + f])
-    swap_first(b_recv)
 
     def over_column(action):
         for dx in (2, 1, 3, 0):
@@ -297,8 +319,26 @@
                     if (dx, dz, dc) != (0, 0, 0):
                         action(lax.rem(x + dx, 4) * 4 + lax.rem(zl + dz, 2) * 2 + lax.rem(c + dc, 2))
 
-    @pl.loop(0, 2)
-    def _(f):
+    def send_pieces(f, phase, pairs_of_refs):
+        over_column(lambda g: [pltpu.make_async_remote_copy(
+            source.at[g], target.at[column], route_send_sems.at[phase + k, f], route_recv_sems.at[phase + k, f],
+            device_id=line + g, device_id_type=LOGICAL).start()
+            for k, (source, target) in enumerate(pairs_of_refs)])
+        for source, target in pairs_of_refs:
+            target[column] = source[column]
+
+    def await_pieces(f, phase, pairs_of_refs):
+        for k, (_, target) in enumerate(pairs_of_refs):
+            finish(target.at[pl.ds(0, 15)], route_recv_sems.at[phase + k, f])
+
+    first_refs = [((r_send.at[0], r_recv), (r_send_rest.at[0], r_recv_rest)),
+                  ((r_send.at[1], r_other), (r_send_rest.at[1], r_other_rest))]
+    second_refs = [((t_send.at[f], t_recv.at[f]), (t_send_rest.at[f], t_recv_rest.at[f])) for f in range(2)]
+
+    fewer = lax.broadcasted_iota(jnp.int32, (32, 128), 1) < 64
+
+    for f in range(2):
+        finish(b_recv.at[f, pl.ds(0, 127 * 8)], recv_sems.at[4 + f])
         for l in range(4):
             cells = pl.ds(l * 128, 128)
             values = jnp.concatenate(
@@ -312,35 +352,26 @@
             g_high[cells, :] = high
             g_low[cells, :] = low
         coarse = dot(rows[...], g_high[...]) + dot(rows[...], g_low[...])
-        for i in range(8):
-            r_send[f * 8 + i, pl.ds(0, 16), :] = coarse[i * PIECE:i * PIECE + 16, 0:128]
-            r_send[f * 8 + i, pl.ds(16, 8), :] = coarse[i * PIECE + 16:(i + 1) * PIECE, 128:256]
-
-    over_column(lambda g: pltpu.make_async_remote_copy(
-        r_send.at[g], r_recv.at[column], send_sems.at[6], recv_sems.at[6],
-        device_id=line + g, device_id_type=LOGICAL).start())
-    r_recv[column] = r_send[column]
-    finish(r_recv.at[pl.ds(0, 15)], recv_sems.at[6])
-
-    lower = lax.broadcasted_iota(jnp.int32, (8, 128), 0) < 4
-
-    @pl.loop(0, 16)
-    def _(g):
-        t_send[g, pl.ds(0, 16), :] = r_recv[order_ref[0, g], pl.ds(0, 16), :]
-        second = r_recv[order_ref[1, g], pl.ds(16, 8), :]
-        third = r_recv[order_ref[2, g], pl.ds(16, 8), :]
-        t_send[g, pl.ds(16, 8), :] = jnp.where(lower, second, third)
-
-    over_column(lambda g: pltpu.make_async_remote_copy(
-        t_send.at[g], t_recv.at[column], send_sems.at[7], recv_sems.at[7],
-        device_id=line + g, device_id_type=LOGICAL).start())
-    t_recv[column] = t_send[column]
-    finish(t_recv.at[pl.ds(0, 15)], recv_sems.at[7])
-    for i in range(16):
-        one_ref[pl.ds(i * 16, 16), :] = t_recv[i, pl.ds(0, 16), :]
-        tail = t_recv[i, pl.ds(16, 8), :]
-        two_ref[pl.ds(i * 4, 4), :] = tail[0:4, 0:64]
-        three_ref[pl.ds(i, 1), :] = tail[4:5, 64:96]
+        r_send[f] = coarse[0:128, 0:128].reshape(16, 8, 128)
+        r_send_rest[f] = jnp.where(fewer, coarse[128:160, 128:256], coarse[160:192, 128:256]).reshape(16, 2, 128)
+        send_pieces(f, 0, first_refs[f])
+
+    for f in range(2):
+        await_pieces(f, 0, first_refs[f])
+        (_, held), (_, held_rest) = first_refs[f]
+
+        @pl.loop(0, 16)
+        def _(g):
+            t_send[f, g] = held[order_smem[0, g]]
+            second, third = held_rest[order_smem[1, g]], held_rest[order_smem[2, g]]
+            t_send_rest[f, g] = jnp.where(fewer[0:2], second, third)
+
+        send_pieces(f, 2, second_refs[f])
+
+    for f in range(2):
+        await_pieces(f, 2, second_refs[f])
+        fine_ref[f] = t_recv[f]
+        rest_ref[f] = t_recv_rest[f]
 
     finish(s_send.at[pl.ds(0, 127)], send_sems.at[0])
 
@@ -349,33 +380,44 @@
         finish(n_send.at[0], send_sems.at[1])
 
     for f in range(2):
-        finish(f_send.at[f, pl.ds(0, 127 * 8)], send_sems.at[2 + f])
-        finish(b_send.at[f, pl.ds(0, 127 * 8)], send_sems.at[4 + f])
-    finish(r_send.at[pl.ds(0, 15)], send_sems.at[6])
-    finish(t_send.at[pl.ds(0, 15)], send_sems.at[7])
+        finish(b_send.at[f, pl.ds(0, 127 * 8)], send_sems.at[6 + f])
+        for k, (whole, rest) in enumerate(((r_send, r_send_rest), (t_send, t_send_rest))):
+            finish(whole.at[f, pl.ds(0, 15)], route_send_sems.at[2 * k, f])
+            finish(rest.at[f, pl.ds(0, 15)], route_send_sems.at[2 * k + 1, f])
+    for f in range(2):
+        for half in range(2):
+            forward_sent(f, half)
+
+
+def finisher(modulus_ref, fine_ref, rest_ref, modulus_hbm, one_ref, two_ref, three_ref, sem):
+    store = pltpu.make_async_copy(modulus_ref, modulus_hbm, sem)
+    store.start()
+    for f in range(2):
+        one_ref[pl.ds(f * 128, 128), :] = fine_ref[f].reshape(128, 128)
+        rest = rest_ref[f]
+        two_ref[pl.ds(f * 32, 32), :] = rest.reshape(32, 128)[:, 0:64]
+        three_ref[pl.ds(f * 8, 8), :] = rest[0:8, 0, 64:96]
+    store.wait()
 
 
 def on_device(white_noise, spectrum, group_table):
     tables, twiddle, pairs, rows = build_tables()
-    anywhere = pl.BlockSpec(memory_space=pl.ANY)
+    hbm = pl.BlockSpec(memory_space=pltpu.HBM)
     vmem = pl.BlockSpec(memory_space=pltpu.VMEM)
-    modulus, one, two, three = pl.pallas_call(
+    modulus_shape = jax.ShapeDtypeStruct((2, CELLS, NZ), F32)
+    modulus, fine, rest = pl.pallas_call(
         kernel,
-        out_shape=(
-            jax.ShapeDtypeStruct((2, CELLS, NZ), F32),
-            jax.ShapeDtypeStruct((256, 128), F32),
-            jax.ShapeDtypeStruct((64, 64), F32),
-            jax.ShapeDtypeStruct((16, 32), F32),
-        ),
-        in_specs=[anywhere, anywhere, pl.BlockSpec(memory_space=pltpu.SMEM)] + [anywhere] * 4,
-        out_specs=(vmem, vmem, vmem, vmem),
+        out_shape=(pltpu.VMEM((2, CELLS, NZ), F32), pltpu.VMEM((2, 16, 8, 128), F32), pltpu.VMEM((2, 16, 2, 128), F32)),
+        in_specs=[hbm] * 7,
+        out_specs=(vmem, vmem, vmem),
         scratch_shapes=[
+            pltpu.SMEM((3, 16), jnp.int32),
             pltpu.VMEM((2, CELLS, NZ), F32),
             pltpu.VMEM((CELLS, NZ), F32),
             pltpu.VMEM((TABLES, 2, 256, 256), BF16),
             pltpu.VMEM((2, 128, CELLS), F32),
             pltpu.VMEM((NZ, 256), BF16),
-            pltpu.VMEM((8 * PIECE, CELLS), BF16),
+            pltpu.VMEM((192, CELLS), BF16),
             pltpu.VMEM((128, 4, 128), F32),
             pltpu.VMEM((2, 128, 4, 128), F32),
             pltpu.VMEM((1, 4, 128), F32),
@@ -392,21 +434,35 @@
             pltpu.VMEM((256, CELLS), BF16),
             pltpu.VMEM((CELLS, 256), BF16),
             pltpu.VMEM((CELLS, 256), BF16),
-            pltpu.VMEM((16, PIECE, 128), F32),
-            pltpu.VMEM((16, PIECE, 128), F32),
-            pltpu.VMEM((16, PIECE, 128), F32),
-            pltpu.VMEM((16, PIECE, 128), F32),
-            pltpu.SemaphoreType.DMA((7,)),
+            *[pltpu.VMEM((*count, 16, size, 128), F32) for size in (8, 2) for count in ((2,), (), ())],
+            *[pltpu.VMEM((2, 16, size, 128), F32) for size in (8, 8, 2, 2)],
             pltpu.SemaphoreType.DMA((8,)),
             pltpu.SemaphoreType.DMA((8,)),
+            pltpu.SemaphoreType.DMA((6,)),
+            pltpu.SemaphoreType.DMA((4, 2)),
+            pltpu.SemaphoreType.DMA((4, 2)),
         ],
         compiler_params=pltpu.CompilerParams(
-            collective_id=0, has_side_effects=True, vmem_limit_bytes=48 << 20),
+            collective_id=0, has_side_effects=True, vmem_limit_bytes=60000000),
         name="moduli",
     )(
         white_noise.reshape(2, CELLS, NZ), spectrum.reshape(CELLS, NZ), group_table,
         jnp.asarray(tables), jnp.asarray(twiddle), jnp.asarray(pairs), jnp.asarray(rows),
     )
+    modulus, one, two, three = pl.pallas_call(
+        finisher,
+        out_shape=(
+            modulus_shape,
+            jax.ShapeDtypeStruct((256, 128), F32),
+            jax.ShapeDtypeStruct((64, 64), F32),
+            jax.ShapeDtypeStruct((16, 32), F32),
+        ),
+        in_specs=[vmem, vmem, vmem],
+        out_specs=(hbm, vmem, vmem, vmem),
+        scratch_shapes=[pltpu.SemaphoreType.DMA],
+        compiler_params=pltpu.CompilerParams(vmem_limit_bytes=4 << 20),
+        name="levels",
+    )(modulus, fine, rest)
     return (
         modulus.reshape(2, CX, CY, NZ),
         one.reshape(2, 8, 16, 128),

time: 66.5 us -> 56.6 us (0.85)
  local copies, waits for them, and re-layouts: 8.65 us -> 0 us
  Pallas kernels: 56.9 us -> 55.8 us
    unnamed x16 -> x0, local copies, waits for them, and re-layouts: 8.65 us -> none
    pallas_call x1 -> x2, Pallas kernels: 56.9 us -> 55.8 us  [the longest x1 54.2 us: on_device(): pl.pallas_call(kernel, out_shape=(pltpu.VMEM((2, CELLS, NZ), F32), pltpu....]
where the time goes in v2:
time: 56.6 us; the launch traced here: 56.5 us
  Pallas kernels  55.8 us (99%)
  between operations  0.64 us (1%)
    pallas_call x1, Pallas kernels, on_device(): pl.pallas_call(kernel, out_shape=(pltpu.VMEM((2, CELLS, NZ), F32), pltpu....  54.2 us
    pallas_call x1, Pallas kernels, on_device(): pl.pallas_call(finisher, out_shape=(modulus_shape, jax.ShapeDtypeStruct((...  1.66 us

profile of v2, /device:TPU:1, one launch (start us, length us, event | category | flops | bytes accessed | tf_op | source)
XLA Modules:
  0.0 56.5 jit_solution(16172066365072201807)
XLA Ops:
  0.6 54.2 %moduli.1 = (f32[2,512,256]{2,1,0:T(8,128)S(1)}, f32[2,16,8,128]{3,2,1,0:T(8,128)S(1)}, f32[2,16,2,128]{3,2,1,0:T(2,128)S(1)}) custom-call(f32[2,512,256]{2,1,0:T(8,128)} %bitcast.6, f32[512,256]{1,0:T(8,128)} %bitcast.7, s32[3,16]{1,0:T(4,128)} %order_hbm.1, bf16[12,2,256,256]{3,2,1,0:T(8,128)(2,1)} %constant.8.clone.tables_hbm, ...), custom_call_target="tpu_custom_call" | custom-call | tf_op jit(solution)/shard_map/moduli/pallas_call | solution.py:408
  54.8 1.7 %levels.1 = (f32[2,512,256]{2,1,0:T(8,128)}, f32[256,128]{1,0:T(8,128)}, f32[64,64]{1,0:T(8,128)}, f32[16,32]{1,0:T(8,128)}) custom-call(f32[2,512,256]{2,1,0:T(8,128)S(1)} %get-tuple-element.11.modulus_ref, f32[2,16,8,128]{3,2,1,0:T(8,128)S(1)} %get-tuple-element.12.fine_ref, f32[2,16,2,128]{3,2,1,0:T(2,128)S(1)} %get-tuple-element.13.rest_ref), custom_call_target="tpu_custom_call" | custom-call | tf_op jit(solution)/shard_map/levels/pallas_call | solution.py:452

commit v3 on v2

--- a/solution.py
+++ b/solution.py
@@ -19,7 +19,7 @@
 NX, NY, NZ = 128, 512, 256
 CX, CY = 16, 32
 CELLS = CX * CY
-T_Z, T_P, T_C, T_CI, T_PI, T_U, TABLES = 0, 1, 2, 6, 10, 11, 12
+T_Z, T_P, T_C, T_PI, T_U, TABLES = 0, 1, 2, 6, 7, 8
 
 
 def wave(products, length, sign):
@@ -51,7 +51,6 @@
     for j2a in range(4):
         inner = 2 * low[:, None] * j2a + 8 * low[:, None] * j2b[None, :] + b[:, None] * m2[None, :]
         tables[T_C + j2a] = applied_left(*wave(inner.T, 32, -1.0)).T
-        tables[T_CI + j2a] = applied_left(*wave(inner, 32, 1.0)).T
     cell_a, cell_b = np.arange(CELLS) // CY, np.arange(CELLS) % CY
     middle = 4 * cell_a[None, :] * j1[:, None] + cell_b[None, :] * m1[:, None]
     twiddle = np.stack(wave(middle, 512, -1.0)).astype(np.float32)
@@ -92,7 +91,7 @@
     noise_hbm, spec_hbm, order_hbm, tables_hbm, twiddle_hbm, pairs_hbm, rows_hbm,
     modulus_ref, fine_ref, rest_ref,
     order_smem, noise, spec, tables, twiddle, pairs, rows,
-    s_send, s_recv, n_send, scale, f_send, f_recv, b_send, b_recv,
+    tables_back, s_send, s_recv, n_send, n_recv, mirrored, reversed_, wrapped, scale, f_send, f_recv, b_send, b_recv,
     y_mid, v_high, v_low, v_back, z_high, z_low, g_high, g_low,
     r_send, r_recv, r_other, r_send_rest, r_recv_rest, r_other_rest, t_send, t_recv, t_send_rest, t_recv_rest,
     load_sems, send_sems, recv_sems, route_send_sems, route_recv_sems,
@@ -156,6 +155,15 @@
         block = jnp.concatenate([spec[pl.ds(s, 16), 128:256] for s in starts], 0)
         n_send[0, jj, :] = block.T[0]
 
+    row = zh * 4 + y
+    on_line = jnp.logical_and(
+        lax.broadcasted_iota(jnp.int32, (4, 128), 0) < 2, lax.broadcasted_iota(jnp.int32, (4, 128), 1) < 16)
+    low_inside, low_line = jnp.where(row >= 4, 0, 1), jnp.where(column >= 8, 0, 1)
+    low_half = jnp.where(jnp.logical_and(on_line, lax.rem(row, 4) == 0), low_line, low_inside) == 1
+    lowest, highest = s_send[0], n_send[0]
+    s_send[0] = jnp.where(low_half, lowest, highest)
+    n_send[0] = jnp.where(low_half, highest, lowest)
+
     loads[1].wait()
     loads[2].wait()
 
@@ -179,12 +187,15 @@
 
     swap_first(f_send)
     pl.semaphore_wait(barrier, 127)
-    over_devices(send(lambda d: s_send.at[d], s_recv.at[0, me], send_sems.at[0], recv_sems.at[0]))
-    s_recv[0, me] = s_send[me]
-
-    @pl.when(me == 0)
+    over_devices(send(lambda d: s_send.at[d], s_recv.at[me], send_sems.at[0], recv_sems.at[0]))
+    s_recv[me] = s_send[me]
+    extra = jnp.logical_and(jnp.logical_and(lax.rem(row, 4) == 0, lax.rem(column, 8) == 0), me != 0)
+
+    @pl.when(extra)
     def _():
-        s_recv[1, 0] = n_send[0]
+        pltpu.make_async_remote_copy(
+            n_send.at[0], n_recv.at[(row // 4) * 2 + column // 8], send_sems.at[1], recv_sems.at[1],
+            device_id=jnp.int32(0), device_id_type=LOGICAL).start()
 
     def send_forward(f, half):
         over_half(send(
@@ -198,29 +209,80 @@
     send_forward(0, 1)
     send_forward(1, 0)
     send_forward(1, 1)
+    for f in range(2):
+        f_recv[f, block_of(me), :] = f_send[f, block_of(me), :]
+
+    finish(s_recv.at[pl.ds(0, 127)], recv_sems.at[0])
+
+    def arrange(plane, load):
+        for j2a in range(4):
+            parts = [load(2 * p_high + j2a // 2, (j2a % 2) * 2 + m2lo) for m2lo in range(2) for p_high in range(4)]
+            scale[plane, j2a] = jnp.concatenate(parts, 0).T
+
+    def received(p, jj):
+        return s_recv[pl.ds(p * 16, 16), jj, :]
+
     @pl.when(me != 0)
     def _():
-        pltpu.make_async_remote_copy(
-            n_send.at[0], s_recv.at[1, me], send_sems.at[1], recv_sems.at[1],
-            device_id=jnp.int32(0), device_id_type=LOGICAL).start()
-
-    for f in range(2):
-        f_recv[f, block_of(me), :] = f_send[f, block_of(me), :]
-
-    finish(s_recv.at[0, pl.ds(0, 127)], recv_sems.at[0])
-
-    def arrange(plane):
-        for j2a in range(4):
-            parts = []
-            for m2lo in range(2):
-                for p_high in range(4):
-                    first = p_high * 32 + (j2a // 2) * 16
-                    parts.append(s_recv[plane, pl.ds(first, 16), (j2a % 2) * 2 + m2lo, :])
-            scale[plane, j2a] = jnp.concatenate(parts, 0).T
-
-    arrange(0)
+        arrange(0, received)
+
+    @pl.when(me == 0)
+    def _():
+        n_recv[0] = n_send[0]
+        finish(n_recv.at[pl.ds(0, 3)], recv_sems.at[1])
+        lanes = lax.broadcasted_iota(jnp.int32, (128, 128), 1)
+        opposite = lax.rem(8 - lax.div(lanes, 16), 8) * 16 + lax.rem(16 - lax.rem(lanes, 16), 16)
+        chosen = jnp.where(lax.broadcasted_iota(jnp.int32, (128, 128), 0) == opposite, 1.0, 0.0).astype(BF16)
+        for jj in range(4):
+            high, low = split(s_recv[:, jj, :])
+            mirrored[:, jj, :] = dot(high, chosen) + dot(low, chosen)
+
+        @pl.loop(0, 8)
+        def _(p):
+            for q in range(16):
+                block = mirrored[p * 16 + q]
+                reversed_[p * 16 + 15 - q] = block
+                wrapped[p * 16 + (16 - q) % 16] = block
+
+        lane = lax.broadcasted_iota(jnp.int32, (16, 128), 1)
+
+        def opposite_block(p, jj):
+            j2lo, m2lo = divmod(jj, 2)
+
+            def over_m(p2, j2):
+                spots = pl.ds(p2 * 16, 16)
+                ends = wrapped[spots, j2 * 2, :] if m2lo == 0 else reversed_[spots, j2 * 2 + 1, :]
+                return jnp.where(lax.rem(lane, 16) == 0, ends, reversed_[spots, j2 * 2 + 1 - m2lo, :])
+
+            ends = over_m((8 - p) % 8, 0) if j2lo == 0 else over_m(7 - p, 1)
+            return jnp.where(lane < 16, ends, over_m(7 - p, 1 - j2lo))
+
+        own = lax.broadcasted_iota(jnp.int32, (16, 128), 0)
+
+        def plane_of(plane):
+            def load(p, jj):
+                block = received(p, jj) if (p >= 4) == (plane == 1) else opposite_block(p, jj)
+                if p % 4 == 0 and jj < 2:
+                    low, high = received(p, jj), opposite_block(p, jj)
+                    if plane == 1:
+                        low, high = high, low
+                    on = jnp.where(own < 8, low, high)
+                    if jj == 0:
+                        spot = jnp.logical_and(lane == 0, own == 8 * (1 - plane))
+                        on = jnp.where(spot, n_recv[(p // 4) * 2 + 1 - plane, pl.ds(0, 1), :], on)
+                    block = jnp.where(lane < 16, on, block)
+                return block
+
+            return load
+
+        for plane in range(2):
+            arrange(plane, plane_of(plane))
+
     for load in loads[3:]:
         load.wait()
+    for j2a in range(4):
+        for k in range(2):
+            tables_back[j2a, k] = tables[T_C + j2a, k].astype(F32).T.astype(BF16)
 
     def send_back(f):
         over_devices(send(
@@ -230,11 +292,6 @@
     @pl.loop(0, 2)
     def _(f):
         finish(f_recv.at[f, pl.ds(0, 127 * 8)], recv_sems.at[2 + f])
-        @pl.when(jnp.logical_and(me == 0, f == 1))
-        def _():
-            finish(s_recv.at[1, pl.ds(0, 127)], recv_sems.at[1])
-            arrange(1)
-
         for part in range(2):
             values = jnp.concatenate([
                 jnp.concatenate([
@@ -271,8 +328,8 @@
                         + dot(high, tables[T_C + j2a, 1]))
             factor = scale[jnp.where(me == 0, f, 0), j2a]
             high, low = split(spectral * jnp.concatenate([factor, factor], 1))
-            v_back[j2a] = (dot(high, tables[T_CI + j2a, 0]) + dot(low, tables[T_CI + j2a, 0])
-                           + dot(high, tables[T_CI + j2a, 1]))
+            v_back[j2a] = (dot(high, tables_back[j2a, 0]) + dot(low, tables_back[j2a, 0])
+                           + dot(high, tables_back[j2a, 1]))
 
         @pl.loop(0, 8)
         def _(n):
@@ -301,13 +358,13 @@
                     b_send[half, pl.ds(row * 4 + part * 2 + l, 128, stride=8), :] = (
                         out[ri * 128:(ri + 1) * 128, l * 128:(l + 1) * 128])
 
+        @pl.when(jnp.logical_and(me == 0, f == 1))
+        def _():
+            send_back(0)
+
         @pl.when(jnp.logical_or(me != 0, f == 1))
         def _():
             send_back(f)
-
-    @pl.when(me == 0)
-    def _():
-        send_back(0)
 
     for f in range(2):
         b_recv[f, block_of(me), :] = b_send[f, block_of(me), :]
@@ -375,7 +432,7 @@
 
     finish(s_send.at[pl.ds(0, 127)], send_sems.at[0])
 
-    @pl.when(me != 0)
+    @pl.when(extra)
     def _():
         finish(n_send.at[0], send_sems.at[1])
 
@@ -418,9 +475,12 @@
             pltpu.VMEM((2, 128, CELLS), F32),
             pltpu.VMEM((NZ, 256), BF16),
             pltpu.VMEM((192, CELLS), BF16),
+            pltpu.VMEM((4, 2, 256, 256), BF16),
             pltpu.VMEM((128, 4, 128), F32),
-            pltpu.VMEM((2, 128, 4, 128), F32),
+            pltpu.VMEM((128, 4, 128), F32),
             pltpu.VMEM((1, 4, 128), F32),
+            pltpu.VMEM((4, 4, 128), F32),
+            *[pltpu.VMEM((128, 4, 128), F32)] * 3,
             pltpu.VMEM((2, 4, 128, 128), F32),
             pltpu.VMEM((2, 1024, 128), F32),
             pltpu.VMEM((2, 1024, 128), F32),

time: 56.6 us -> 55.2 us (0.975)
  Pallas kernels: 55.8 us -> 54.4 us
    pallas_call x1, Pallas kernels: 54.2 us -> 52.8 us  [on_device(): pl.pallas_call(kernel, out_shape=(pltpu.VMEM((2, CELLS, NZ), F32), pltpu....]
where the time goes in v3:
time: 55.2 us; the launch traced here: 55.1 us
  Pallas kernels  54.4 us (99%)
  between operations  0.64 us (1%)
    pallas_call x1, Pallas kernels, on_device(): pl.pallas_call(kernel, out_shape=(pltpu.VMEM((2, CELLS, NZ), F32), pltpu....  52.8 us
    pallas_call x1, Pallas kernels, on_device(): pl.pallas_call(finisher, out_shape=(modulus_shape, jax.ShapeDtypeStruct((...  1.66 us

profile of v3, /device:TPU:1, one launch (start us, length us, event | category | flops | bytes accessed | tf_op | source)
XLA Modules:
  0.0 55.1 jit_solution(14020514231080975824)
XLA Ops:
  0.6 52.8 %moduli.1 = (f32[2,512,256]{2,1,0:T(8,128)S(1)}, f32[2,16,8,128]{3,2,1,0:T(8,128)S(1)}, f32[2,16,2,128]{3,2,1,0:T(2,128)S(1)}) custom-call(f32[2,512,256]{2,1,0:T(8,128)} %bitcast.6, f32[512,256]{1,0:T(8,128)} %bitcast.7, s32[3,16]{1,0:T(4,128)} %order_hbm.1, bf16[8,2,256,256]{3,2,1,0:T(8,128)(2,1)} %constant.8.clone.tables_hbm, ...), custom_call_target="tpu_custom_call" | custom-call | tf_op jit(solution)/shard_map/moduli/pallas_call | solution.py:465
  53.4 1.7 %levels.1 = (f32[2,512,256]{2,1,0:T(8,128)}, f32[256,128]{1,0:T(8,128)}, f32[64,64]{1,0:T(8,128)}, f32[16,32]{1,0:T(8,128)}) custom-call(f32[2,512,256]{2,1,0:T(8,128)S(1)} %get-tuple-element.11.modulus_ref, f32[2,16,8,128]{3,2,1,0:T(8,128)S(1)} %get-tuple-element.12.fine_ref, f32[2,16,2,128]{3,2,1,0:T(2,128)S(1)} %get-tuple-element.13.rest_ref), custom_call_target="tpu_custom_call" | custom-call | tf_op jit(solution)/shard_map/levels/pallas_call | solution.py:512

commit v4 on v3

--- a/solution.py
+++ b/solution.py
@@ -92,7 +92,7 @@
     modulus_ref, fine_ref, rest_ref,
     order_smem, noise, spec, tables, twiddle, pairs, rows,
     tables_back, s_send, s_recv, n_send, n_recv, mirrored, reversed_, wrapped, scale, f_send, f_recv, b_send, b_recv,
-    y_mid, v_high, v_low, v_back, z_high, z_low, g_high, g_low,
+    y_mid, v_high, v_low, v_back, z_high, z_low, w_high, w_low, g_high, g_low,
     r_send, r_recv, r_other, r_send_rest, r_recv_rest, r_other_rest, t_send, t_recv, t_send_rest, t_recv_rest,
     load_sems, send_sems, recv_sems, route_send_sems, route_recv_sems,
 ):
@@ -207,8 +207,6 @@
 
     send_forward(0, 0)
     send_forward(0, 1)
-    send_forward(1, 0)
-    send_forward(1, 1)
     for f in range(2):
         f_recv[f, block_of(me), :] = f_send[f, block_of(me), :]
 
@@ -278,6 +276,8 @@
         for plane in range(2):
             arrange(plane, plane_of(plane))
 
+    send_forward(1, 0)
+    send_forward(1, 1)
     for load in loads[3:]:
         load.wait()
     for j2a in range(4):
@@ -398,9 +398,13 @@
         finish(b_recv.at[f, pl.ds(0, 127 * 8)], recv_sems.at[4 + f])
         for l in range(4):
             cells = pl.ds(l * 128, 128)
-            values = jnp.concatenate(
-                [b_recv[f, pl.ds(ri * 4 + l, 128, stride=8), :].T for ri in range(2)], 1)
-            high, low = split(values)
+            for ri in range(2):
+                high, low = split(b_recv[f, pl.ds(ri * 4 + l, 128, stride=8), :].T)
+                w_high[cells, ri * 128:(ri + 1) * 128] = high
+                w_low[cells, ri * 128:(ri + 1) * 128] = low
+        for part in range(2):
+            cells = pl.ds(part * 256, 256)
+            high, low = w_high[cells, :], w_low[cells, :]
             fields = dot(high, tables[T_U, 0]) + dot(low, tables[T_U, 0]) + dot(high, tables[T_U, 1])
             modulus = jnp.exp(0.5 * fields)
             modulus_ref[f, cells, :] = modulus
@@ -446,15 +450,20 @@
             forward_sent(f, half)
 
 
-def finisher(modulus_ref, fine_ref, rest_ref, modulus_hbm, one_ref, two_ref, three_ref, sem):
-    store = pltpu.make_async_copy(modulus_ref, modulus_hbm, sem)
-    store.start()
-    for f in range(2):
-        one_ref[pl.ds(f * 128, 128), :] = fine_ref[f].reshape(128, 128)
+def finisher(modulus_ref, fine_ref, rest_ref, modulus_hbm, one_hbm, two_hbm, three_hbm, two, three, sems):
+    stores = [
+        pltpu.make_async_copy(source, target, sems.at[k]) for k, (source, target) in enumerate((
+            (modulus_ref, modulus_hbm), (fine_ref, one_hbm), (two, two_hbm), (three, three_hbm)))]
+    stores[0].start()
+    stores[1].start()
+    for f in range(2):
         rest = rest_ref[f]
-        two_ref[pl.ds(f * 32, 32), :] = rest.reshape(32, 128)[:, 0:64]
-        three_ref[pl.ds(f * 8, 8), :] = rest[0:8, 0, 64:96]
-    store.wait()
+        two[pl.ds(f * 32, 32), :] = rest.reshape(32, 128)[:, 0:64]
+        three[pl.ds(f * 8, 8), :] = rest[0:8, 0, 64:96]
+    stores[2].start()
+    stores[3].start()
+    for store in stores:
+        store.wait()
 
 
 def on_device(white_noise, spectrum, group_table):
@@ -492,8 +501,7 @@
             pltpu.VMEM((4, 128, 256), F32),
             pltpu.VMEM((256, CELLS), BF16),
             pltpu.VMEM((256, CELLS), BF16),
-            pltpu.VMEM((CELLS, 256), BF16),
-            pltpu.VMEM((CELLS, 256), BF16),
+            *[pltpu.VMEM((CELLS, 256), BF16)] * 4,
             *[pltpu.VMEM((*count, 16, size, 128), F32) for size in (8, 2) for count in ((2,), (), ())],
             *[pltpu.VMEM((2, 16, size, 128), F32) for size in (8, 8, 2, 2)],
             pltpu.SemaphoreType.DMA((8,)),
@@ -513,13 +521,13 @@
         finisher,
         out_shape=(
             modulus_shape,
-            jax.ShapeDtypeStruct((256, 128), F32),
+            jax.ShapeDtypeStruct((2, 16, 8, 128), F32),
             jax.ShapeDtypeStruct((64, 64), F32),
             jax.ShapeDtypeStruct((16, 32), F32),
         ),
         in_specs=[vmem, vmem, vmem],
-        out_specs=(hbm, vmem, vmem, vmem),
-        scratch_shapes=[pltpu.SemaphoreType.DMA],
+        out_specs=(hbm, hbm, hbm, hbm),
+        scratch_shapes=[pltpu.VMEM((64, 64), F32), pltpu.VMEM((16, 32), F32), pltpu.SemaphoreType.DMA((4,))],
         compiler_params=pltpu.CompilerParams(vmem_limit_bytes=4 << 20),
         name="levels",
     )(modulus, fine, rest)

time: 55.2 us -> 52.6 us (0.953)
  Pallas kernels: 54.4 us -> 51.8 us
    pallas_call x1, Pallas kernels: 52.8 us -> 50.8 us  [on_device(): pl.pallas_call(kernel, out_shape=(pltpu.VMEM((2, CELLS, NZ), F32), pltpu....]
    pallas_call x1, Pallas kernels: 1.66 us -> 1.05 us  [on_device(): pl.pallas_call(finisher, out_shape=(modulus_shape, jax.ShapeDtypeStruct((...]
where the time goes in v4:
time: 52.6 us; the launch traced here: 52.4 us
  Pallas kernels  51.8 us (98%)
  between operations  0.64 us (1%)
    pallas_call x1, Pallas kernels, on_device(): pl.pallas_call(kernel, out_shape=(pltpu.VMEM((2, CELLS, NZ), F32), pltpu....  50.8 us

profile of v4, /device:TPU:1, one launch (start us, length us, event | category | flops | bytes accessed | tf_op | source)
XLA Modules:
  0.0 52.4 jit_solution(15841844918174151743)
XLA Ops:
  0.6 50.8 %moduli.1 = (f32[2,512,256]{2,1,0:T(8,128)S(1)}, f32[2,16,8,128]{3,2,1,0:T(8,128)S(1)}, f32[2,16,2,128]{3,2,1,0:T(2,128)S(1)}) custom-call(f32[2,512,256]{2,1,0:T(8,128)} %bitcast.6, f32[512,256]{1,0:T(8,128)} %bitcast.7, s32[3,16]{1,0:T(4,128)} %order_hbm.1, bf16[8,2,256,256]{3,2,1,0:T(8,128)(2,1)} %constant.8.clone.tables_hbm, ...), custom_call_target="tpu_custom_call" | custom-call | tf_op jit(solution)/shard_map/moduli/pallas_call | solution.py:474
  51.4 1.0 %levels.1 = (f32[2,512,256]{2,1,0:T(8,128)}, f32[2,16,8,128]{3,2,1,0:T(8,128)}, f32[64,64]{1,0:T(8,128)}, f32[16,32]{1,0:T(8,128)}) custom-call(f32[2,512,256]{2,1,0:T(8,128)S(1)} %get-tuple-element.11.modulus_ref, f32[2,16,8,128]{3,2,1,0:T(8,128)S(1)} %get-tuple-element.12.fine_ref, f32[2,16,2,128]{3,2,1,0:T(2,128)S(1)} %get-tuple-element.13.rest_ref), custom_call_target="tpu_custom_call" | custom-call | tf_op jit(solution)/shard_map/levels/pallas_call | solution.py:520

commit v5 on v4

--- a/solution.py
+++ b/solution.py
@@ -108,9 +108,11 @@
         (tables_hbm.at[pl.ds(1, TABLES - 1)], tables.at[pl.ds(1, TABLES - 1)]),
         (twiddle_hbm, twiddle), (pairs_hbm, pairs), (rows_hbm, rows), (order_hbm, order_smem),
     )):
-        load = pltpu.make_async_copy(source, target, load_sems.at[k])
+        loads.append(pltpu.make_async_copy(source, target, load_sems.at[k]))
+    for load in loads[:3]:
         load.start()
-        loads.append(load)
+
+    spots = [(lax.rem(y + dy, 4) * 16 + lax.rem(x + dx, 4) * 4) for dy in (2, 1, 3, 0) for dx in (2, 1, 3, 0)]
 
     def over_half(action, half):
         core = lax.rem(c + 1 - half, 2)
@@ -118,12 +120,9 @@
         def group(s, skip):
             z2 = lax.rem(z + ordered(s), 4)
             base = (z2 // 2) * 64 + lax.rem(z2, 2) * 2 + core
-            ys = [lax.rem(y + ordered(lax.rem(s + t, 4)), 4) * 16 for t in range(4)]
-            xs = [lax.rem(x + ordered(lax.rem(s + t, 4)), 4) * 4 for t in range(4)]
-            for t in range(4):
-                for u in range(4):
-                    if not (skip and t == 0 and u == 0):
-                        action(base + ys[t] + xs[u])
+            for k, spot in enumerate(spots):
+                if not (skip and k == 15):
+                    action(base + spot)
 
         @pl.loop(0, 4 - half)
         def _(s):
@@ -138,6 +137,9 @@
 
     barrier = pltpu.get_barrier_semaphore()
     over_devices(lambda d: pl.semaphore_signal(barrier, 1, device_id=d, device_id_type=LOGICAL))
+
+    for load in loads[3:]:
+        load.start()
 
     def send(source, target, send_sem, recv_sem):
         return lambda d: pltpu.make_async_remote_copy(

time: 52.6 us -> 52.1 us (level)
  no operation moved by 1% of the time
where the time goes in v5:
time: 52.1 us; the launch traced here: 52 us
  Pallas kernels  51.4 us (99%)
  between operations  0.64 us (1%)
    pallas_call x1, Pallas kernels, on_device(): pl.pallas_call(kernel, out_shape=(pltpu.VMEM((2, CELLS, NZ), F32), pltpu....  50.3 us
    pallas_call x1, Pallas kernels, on_device(): pl.pallas_call(finisher, out_shape=(modulus_shape, jax.ShapeDtypeStruct((...  1.05 us

profile of v5, /device:TPU:1, one launch (start us, length us, event | category | flops | bytes accessed | tf_op | source)
XLA Modules:
  0.0 52.0 jit_solution(10281372405080482694)
XLA Ops:
  0.6 50.3 %moduli.1 = (f32[2,512,256]{2,1,0:T(8,128)S(1)}, f32[2,16,8,128]{3,2,1,0:T(8,128)S(1)}, f32[2,16,2,128]{3,2,1,0:T(2,128)S(1)}) custom-call(f32[2,512,256]{2,1,0:T(8,128)} %bitcast.6, f32[512,256]{1,0:T(8,128)} %bitcast.7, s32[3,16]{1,0:T(4,128)} %order_hbm.1, bf16[8,2,256,256]{3,2,1,0:T(8,128)(2,1)} %constant.8.clone.tables_hbm, ...), custom_call_target="tpu_custom_call" | custom-call | tf_op jit(solution)/shard_map/moduli/pallas_call | solution.py:476
  51.0 1.0 %levels.1 = (f32[2,512,256]{2,1,0:T(8,128)}, f32[2,16,8,128]{3,2,1,0:T(8,128)}, f32[64,64]{1,0:T(8,128)}, f32[16,32]{1,0:T(8,128)}) custom-call(f32[2,512,256]{2,1,0:T(8,128)S(1)} %get-tuple-element.11.modulus_ref, f32[2,16,8,128]{3,2,1,0:T(8,128)S(1)} %get-tuple-element.12.fine_ref, f32[2,16,2,128]{3,2,1,0:T(2,128)S(1)} %get-tuple-element.13.rest_ref), custom_call_target="tpu_custom_call" | custom-call | tf_op jit(solution)/shard_map/levels/pallas_call | solution.py:522

commit v6 on v5

--- a/solution.py
+++ b/solution.py
@@ -287,9 +287,10 @@
             tables_back[j2a, k] = tables[T_C + j2a, k].astype(F32).T.astype(BF16)
 
     def send_back(f):
-        over_devices(send(
-            lambda d: b_send.at[f, block_of(d)], b_recv.at[f, block_of(me)],
-            send_sems.at[6 + f], recv_sems.at[4 + f]))
+        for half in (1, 0):
+            over_half(send(
+                lambda d: b_send.at[f, block_of(d)], b_recv.at[f, block_of(me)],
+                send_sems.at[6 + f], recv_sems.at[4 + f]), half)
 
     @pl.loop(0, 2)
     def _(f):

time: 52.1 us -> 51.1 us (0.981)
  Pallas kernels: 51.4 us -> 50.4 us
    pallas_call x1, Pallas kernels: 50.3 us -> 49.3 us  [on_device(): pl.pallas_call(kernel, out_shape=(pltpu.VMEM((2, CELLS, NZ), F32), pltpu....]
where the time goes in v6:
time: 51.1 us; the launch traced here: 51 us
  Pallas kernels  50.4 us (99%)
  between operations  0.64 us (1%)
    pallas_call x1, Pallas kernels, on_device(): pl.pallas_call(kernel, out_shape=(pltpu.VMEM((2, CELLS, NZ), F32), pltpu....  49.3 us
    pallas_call x1, Pallas kernels, on_device(): pl.pallas_call(finisher, out_shape=(modulus_shape, jax.ShapeDtypeStruct((...  1.05 us

profile of v6, /device:TPU:1, one launch (start us, length us, event | category | flops | bytes accessed | tf_op | source)
XLA Modules:
  0.0 51.0 jit_solution(7331771575759643862)
XLA Ops:
  0.6 49.3 %moduli.1 = (f32[2,512,256]{2,1,0:T(8,128)S(1)}, f32[2,16,8,128]{3,2,1,0:T(8,128)S(1)}, f32[2,16,2,128]{3,2,1,0:T(2,128)S(1)}) custom-call(f32[2,512,256]{2,1,0:T(8,128)} %bitcast.6, f32[512,256]{1,0:T(8,128)} %bitcast.7, s32[3,16]{1,0:T(4,128)} %order_hbm.1, bf16[8,2,256,256]{3,2,1,0:T(8,128)(2,1)} %constant.8.clone.tables_hbm, ...), custom_call_target="tpu_custom_call" | custom-call | tf_op jit(solution)/shard_map/moduli/pallas_call | solution.py:477
  50.0 1.0 %levels.1 = (f32[2,512,256]{2,1,0:T(8,128)}, f32[2,16,8,128]{3,2,1,0:T(8,128)}, f32[64,64]{1,0:T(8,128)}, f32[16,32]{1,0:T(8,128)}) custom-call(f32[2,512,256]{2,1,0:T(8,128)S(1)} %get-tuple-element.11.modulus_ref, f32[2,16,8,128]{3,2,1,0:T(8,128)S(1)} %get-tuple-element.12.fine_ref, f32[2,16,2,128]{3,2,1,0:T(2,128)S(1)} %get-tuple-element.13.rest_ref), custom_call_target="tpu_custom_call" | custom-call | tf_op jit(solution)/shard_map/levels/pallas_call | solution.py:523

commit v7 on v6

--- a/solution.py
+++ b/solution.py
@@ -189,7 +189,8 @@
 
     swap_first(f_send)
     pl.semaphore_wait(barrier, 127)
-    over_devices(send(lambda d: s_send.at[d], s_recv.at[me], send_sems.at[0], recv_sems.at[0]))
+    for half in (1, 0):
+        over_half(send(lambda d: s_send.at[d], s_recv.at[me], send_sems.at[0], recv_sems.at[0]), half)
     s_recv[me] = s_send[me]
     extra = jnp.logical_and(jnp.logical_and(lax.rem(row, 4) == 0, lax.rem(column, 8) == 0), me != 0)
 
@@ -207,8 +208,8 @@
     def forward_sent(f, half):
         finish(f_send.at[f, pl.ds(0, (64 - half) * 8)], send_sems.at[2 + 2 * f + half])
 
+    send_forward(0, 1)
     send_forward(0, 0)
-    send_forward(0, 1)
     for f in range(2):
         f_recv[f, block_of(me), :] = f_send[f, block_of(me), :]
 

time: 51.1 us -> 52.6 us (1.029)
  Pallas kernels: 50.4 us -> 51.8 us
    pallas_call x1, Pallas kernels: 49.3 us -> 50.8 us  [on_device(): pl.pallas_call(kernel, out_shape=(pltpu.VMEM((2, CELLS, NZ), F32), pltpu....]
where the time goes in v7:
time: 52.6 us; the launch traced here: 52.5 us
  Pallas kernels  51.8 us (98%)
  between operations  0.64 us (1%)
    pallas_call x1, Pallas kernels, on_device(): pl.pallas_call(kernel, out_shape=(pltpu.VMEM((2, CELLS, NZ), F32), pltpu....  50.8 us

profile of v7, /device:TPU:1, one launch (start us, length us, event | category | flops | bytes accessed | tf_op | source)
XLA Modules:
  0.0 52.5 jit_solution(13314230580848460267)
XLA Ops:
  0.6 50.8 %moduli.1 = (f32[2,512,256]{2,1,0:T(8,128)S(1)}, f32[2,16,8,128]{3,2,1,0:T(8,128)S(1)}, f32[2,16,2,128]{3,2,1,0:T(2,128)S(1)}) custom-call(f32[2,512,256]{2,1,0:T(8,128)} %bitcast.6, f32[512,256]{1,0:T(8,128)} %bitcast.7, s32[3,16]{1,0:T(4,128)} %order_hbm.1, bf16[8,2,256,256]{3,2,1,0:T(8,128)(2,1)} %constant.8.clone.tables_hbm, ...), custom_call_target="tpu_custom_call" | custom-call | tf_op jit(solution)/shard_map/moduli/pallas_call | solution.py:478
  51.4 1.0 %levels.1 = (f32[2,512,256]{2,1,0:T(8,128)}, f32[2,16,8,128]{3,2,1,0:T(8,128)}, f32[64,64]{1,0:T(8,128)}, f32[16,32]{1,0:T(8,128)}) custom-call(f32[2,512,256]{2,1,0:T(8,128)S(1)} %get-tuple-element.11.modulus_ref, f32[2,16,8,128]{3,2,1,0:T(8,128)S(1)} %get-tuple-element.12.fine_ref, f32[2,16,2,128]{3,2,1,0:T(2,128)S(1)} %get-tuple-element.13.rest_ref), custom_call_target="tpu_custom_call" | custom-call | tf_op jit(solution)/shard_map/levels/pallas_call | solution.py:524
